TPU v7x, 256 devices: a whole 4x4x8 slice. The times are simulated.
256 devices in a mesh: pulse: 8 (over y_lo, x), tile: 32 (over z, y_hi, core).
Axes of the slice: x: 4, y: 4 (y_hi: 2, y_lo: 2; y = y_hi * 2 + y_lo), z: 8, core: 2. Of those that a mesh axis runs over, the one named last changes fastest.
Arguments:
- pulses: bfloat16 [4096, 2, 32768], P(None, None, ('pulse', 'tile')), may hold values from -6 to 6
- steering: bfloat16 [2, 128, 128], replicated, may hold values from -0.375 to 0.375
- merge_re: bfloat16 [3, 256, 256], replicated, may hold values from -0.25 to 0.25
- merge_im: bfloat16 [3, 256, 256], replicated, may hold values from -0.25 to 0.25
- range_shift: int32 [3, 2, 128], replicated, may hold values from -8 to 8
- image_map: bfloat16 [8, 32, 2, 128, 512], P('pulse', 'tile'), may hold values from -0.0234375 to 0.0234375
Outputs:
- image: float32 [4096, 1024], P(('pulse', 'tile'))
All inputs are finite; a program needn't handle non-finite values.
Results may differ from a plain program's by a relative error of at most 0.0057.
Values may be sent and summed in bfloat16 or wider, within the bound.
A program may use at most 64 MiB of HBM per device.

v0:
```python
import jax
import jax.numpy as jnp
from jax import lax
from jax.sharding import PartitionSpec as P

SHIFT = 8


def partner_2(value, axis, apart):
    mask = 2**apart
    pairs = [(source, source ^ mask) for source in range(lax.axis_size(axis))]
    return lax.ppermute(value, axis, pairs)


def in_blocks(array, dim, length):
    before, after = (array.shape[:dim], array.shape[dim + 1 :])
    return jnp.moveaxis(array.reshape(*before, length, -1, *after), dim, 0)


def summed_on_arrival(array, axis, dim):
    length = lax.axis_size(axis)
    pieces = lax.all_to_all(in_blocks(array, dim, length), axis, 0, 0, tiled=True)
    return jnp.sum(pieces, axis=0)


def complex_block(real_part, imag_part):
    upper_half = jnp.concatenate([real_part, imag_part], axis=1)
    lower_half = jnp.concatenate([-imag_part, real_part], axis=1)
    return jnp.concatenate([upper_half, lower_half], axis=0)


def shift_rows(beam_rows, shift_table):
    range_rows = beam_rows.shape[0]
    doubled = jnp.concatenate([shift_table, shift_table])
    padded = jnp.pad(beam_rows, ((SHIFT, SHIFT), (0, 0)))
    result = jnp.zeros_like(beam_rows)
    for offset in range(-SHIFT, SHIFT + 1):
        window = padded[SHIFT + offset : SHIFT + offset + range_rows]
        result = jnp.where(doubled[None, :] == offset, window, result)
    return result


def body(pulses, steering, merge_re, merge_im, range_shift, image_map):
    range_rows = pulses.shape[0]
    beam_count = steering.shape[2]
    group_count = lax.axis_size("pulse")
    tile_count = lax.axis_size("tile")
    pulse_rows = pulses.reshape(range_rows, -1)
    current = jnp.dot(
        pulse_rows, complex_block(steering[0], steering[1]), preferred_element_type=jnp.float32
    ).astype(jnp.bfloat16)
    position = lax.axis_index("tile")
    for merge_level in range(merge_re.shape[0]):
        partner = partner_2(current, "tile", merge_level)
        half_bit = position >> merge_level & 1
        is_upper = half_bit == 1
        lower_src = jnp.where(is_upper, partner, current)
        upper_src = jnp.where(is_upper, current, partner)
        shifted_lower = shift_rows(lower_src, range_shift[merge_level, 0])
        shifted_upper = shift_rows(upper_src, range_shift[merge_level, 1])
        combined = jnp.concatenate(
            [
                shifted_lower[:, :beam_count],
                shifted_upper[:, :beam_count],
                shifted_lower[:, beam_count:],
                shifted_upper[:, beam_count:],
            ],
            axis=1,
        )
        weight_re = lax.dynamic_slice_in_dim(
            merge_re[merge_level], half_bit * beam_count, beam_count, 1
        )
        weight_im = lax.dynamic_slice_in_dim(
            merge_im[merge_level], half_bit * beam_count, beam_count, 1
        )
        current = jnp.dot(
            combined, complex_block(weight_re, weight_im), preferred_element_type=jnp.float32
        ).astype(jnp.bfloat16)
    block_rows = range_rows // (group_count * tile_count)
    arranged = current.reshape(1, group_count, tile_count, block_rows, 2 * beam_count)
    received = lax.all_to_all(arranged, "tile", split_axis=2, concat_axis=0, tiled=True)
    received = received.reshape(tile_count, group_count * block_rows, 2 * beam_count)
    piece = lax.all_gather(image_map, "tile", axis=1, tiled=True)
    blocks = jax.vmap(complex_block)(piece[0][:, 0], piece[0][:, 1])
    partial_rows = jnp.einsum("jrk,jkx->rx", received, blocks, preferred_element_type=jnp.float32)
    result = summed_on_arrival(partial_rows, "pulse", 0)
    return result


def solution(mesh):
    placed = (
        P(None, None, ("pulse", "tile")),
        P(),
        P(),
        P(),
        P(),
        P("pulse", "tile", None, None, None),
    )
    return jax.shard_map(
        body, mesh=mesh, in_specs=placed, out_specs=P(("pulse", "tile"), None), check_vma=False
    )
```

profile of v0, /device:TPU:1, one launch (start us, length us, event | category | flops | bytes accessed | tf_op | source)
XLA Modules:
  0.0 322.8 jit_solution(17331129993436597664)
XLA Ops:
  8.1 2.4 fusion.9
  10.5 3.3 %collective-permute-start = (bf16[4096,256]{0,1:T(8,128)(2,1)S(1)}, bf16[4096,256]{0,1:T(8,128)(2,1)}, u32[]{:S(2)}, u32[]{:S(2)}) collective-permute-start(bf16[4096,256]{0,1:T(8,128)(2,1)S(1)} %fusion.9), channel_id=1, source_target_pairs={{0,1},{1,0},{2,3},{3,2},{4,5},{5,4},{6,7},{7,6},{8,9},{9,8},{10,11... | collective-permute-start | bytes 6291464 | tf_op jit(solution)/shard_map/ppermute | solution.py:12
  14.1 3.6 %collective-permute-done = bf16[4096,256]{0,1:T(8,128)(2,1)} collective-permute-done((bf16[4096,256]{0,1:T(8,128)(2,1)S(1)}, bf16[4096,256]{0,1:T(8,128)(2,1)}, u32[]{:S(2)}, u32[]{:S(2)}) %collective-permute-start) | collective-permute-done | bytes 2097184 | tf_op jit(solution)/shard_map/ppermute | solution.py:12
  17.7 1.9 broadcast_select_fusion.1
  19.6 16.6 %select_select_fusion.4 = bf16[4096,256]{0,1:T(8,128)(2,1)S(1)} fusion(bf16[4096,256]{0,1:T(8,128)(2,1)S(1)} %get-tuple-element.18, pred[256]{0:T(512)(128)(4,1)S(1)} %get-tuple-element.145, pred[256]{0:T(512)(128)(4,1)S(1)} %get-tuple-element.140, pred[256]{0:T(512)(128)(4,1)S(1)} %get-tuple-element.139, pred[256]{0:T(512)(128)(4,1)S(1)} %get-tuple-element.138, ...), kind=kLoop, calls=%fused_computation.60 | loop fusion | flops 17825792 | bytes 4198656 | tf_op jit(solution)/shard_map/jit(_where)/select_n | solution.py:39
  36.4 16.6 %select_select_fusion.5 = bf16[4096,256]{0,1:T(8,128)(2,1)S(1)} fusion(bf16[4096,256]{0,1:T(8,128)(2,1)S(1)} %get-tuple-element.17, pred[256]{0:T(512)(128)(4,1)S(1)} %get-tuple-element.146, pred[256]{0:T(512)(128)(4,1)S(1)} %get-tuple-element.124, pred[256]{0:T(512)(128)(4,1)S(1)} %get-tuple-element.123, pred[256]{0:T(512)(128)(4,1)S(1)} %get-tuple-element.122, ...), kind=kLoop, calls=%fused_computation.65 | loop fusion | flops 17825792 | bytes 4198656 | tf_op jit(solution)/shard_map/jit(_where)/select_n | solution.py:39
  53.2 1.6 convolution_convert_fusion.2
  56.5 49.8 %collective-permute-done.1 = bf16[4096,256]{0,1:T(8,128)(2,1)} collective-permute-done((bf16[4096,256]{0,1:T(8,128)(2,1)S(1)}, bf16[4096,256]{0,1:T(8,128)(2,1)}, u32[]{:S(2)}, u32[]{:S(2)}) %collective-permute-start.1) | collective-permute-done | bytes 2097184 | tf_op jit(solution)/shard_map/ppermute | solution.py:12
  106.3 1.9 broadcast_select_fusion.3
  108.1 16.6 %select_select_fusion.2 = bf16[4096,256]{0,1:T(8,128)(2,1)S(1)} fusion(bf16[4096,256]{0,1:T(8,128)(2,1)S(1)} %get-tuple-element.16, pred[256]{0:T(512)(128)(4,1)S(1)} %get-tuple-element.143, pred[256]{0:T(512)(128)(4,1)S(1)} %get-tuple-element.108, pred[256]{0:T(512)(128)(4,1)S(1)} %get-tuple-element.107, pred[256]{0:T(512)(128)(4,1)S(1)} %get-tuple-element.106, ...), kind=kLoop, calls=%fused_computation.50 | loop fusion | flops 17825792 | bytes 4198656 | tf_op jit(solution)/shard_map/jit(_where)/select_n | solution.py:39
  124.9 16.6 %select_select_fusion.3 = bf16[4096,256]{0,1:T(8,128)(2,1)S(1)} fusion(bf16[4096,256]{0,1:T(8,128)(2,1)S(1)} %get-tuple-element.15, pred[256]{0:T(512)(128)(4,1)S(1)} %get-tuple-element.144, pred[256]{0:T(512)(128)(4,1)S(1)} %get-tuple-element.92, pred[256]{0:T(512)(128)(4,1)S(1)} %get-tuple-element.91, pred[256]{0:T(512)(128)(4,1)S(1)} %get-tuple-element.90, ...), kind=kLoop, calls=%fused_computation.55 | loop fusion | flops 17825792 | bytes 4198656 | tf_op jit(solution)/shard_map/jit(_where)/select_n | solution.py:39
  141.7 1.6 convolution_convert_fusion.1
  143.8 54.0 %collective-permute-done.2 = bf16[4096,256]{0,1:T(8,128)(2,1)} collective-permute-done((bf16[4096,256]{0,1:T(8,128)(2,1)S(1)}, bf16[4096,256]{0,1:T(8,128)(2,1)}, u32[]{:S(2)}, u32[]{:S(2)}) %collective-permute-start.2) | collective-permute-done | bytes 2097184 | tf_op jit(solution)/shard_map/ppermute | solution.py:12
  197.8 1.9 broadcast_select_fusion.5
  199.7 16.6 %select_select_fusion = bf16[4096,256]{0,1:T(8,128)(2,1)S(1)} fusion(bf16[4096,256]{0,1:T(8,128)(2,1)S(1)} %get-tuple-element.14, pred[256]{0:T(512)(128)(4,1)S(1)} %get-tuple-element.141, pred[256]{0:T(512)(128)(4,1)S(1)} %get-tuple-element.76, pred[256]{0:T(512)(128)(4,1)S(1)} %get-tuple-element.75, pred[256]{0:T(512)(128)(4,1)S(1)} %get-tuple-element.74, ...), kind=kLoop, calls=%fused_computation.40 | loop fusion | flops 17825792 | bytes 4198656 | tf_op jit(solution)/shard_map/jit(_where)/select_n | solution.py:39
  216.5 16.6 %select_select_fusion.1 = bf16[4096,256]{0,1:T(8,128)(2,1)S(1)} fusion(bf16[4096,256]{0,1:T(8,128)(2,1)S(1)} %get-tuple-element.13, pred[256]{0:T(512)(128)(4,1)S(1)} %get-tuple-element.142, pred[256]{0:T(512)(128)(4,1)S(1)} %get-tuple-element.60, pred[256]{0:T(512)(128)(4,1)S(1)} %get-tuple-element.59, pred[256]{0:T(512)(128)(4,1)S(1)} %get-tuple-element.58, ...), kind=kLoop, calls=%fused_computation.45 | loop fusion | flops 17825792 | bytes 4198656 | tf_op jit(solution)/shard_map/jit(_where)/select_n | solution.py:39
  233.3 1.6 convolution_convert_fusion
  234.9 1.6 copy.18
  236.4 7.1 %all-to-all-start = ((bf16[1,8,32,16,256]{4,3,1,0,2:T(8,128)(2,1)}), bf16[1,8,32,16,256]{4,3,1,0,2:T(8,128)(2,1)S(1)}, u32[]{:S(2)}, u32[]{:S(2)}) async-start(bf16[1,8,32,16,256]{4,3,1,0,2:T(8,128)(2,1)} %copy.18), calls=%async_computation | async-start | bytes 4194304 | tf_op jit(solution)/shard_map/all_to_all | solution.py:81
  243.6 4.7 %fusion.73 = bf16[32,128,512]{2,1,0:T(8,128)(2,1)} fusion(bf16[32,2,128,512]{3,2,0,1:T(8,128)(2,1)} %bitcast.73), kind=kLoop, calls=%fused_computation.233 | loop fusion | flops 2097152 | bytes 8388608 | tf_op jit(solution)/shard_map/vmap()/neg | solution.py:28
  249.7 3.7 %slice_bitcast_fusion = (bf16[32,128,512]{2,1,0:T(8,128)(2,1)}, bf16[32,128,512]{2,1,0:T(8,128)(2,1)}) fusion(bf16[32,2,128,512]{3,2,0,1:T(8,128)(2,1)S(1)} %bitcast.74), kind=kLoop, calls=%fused_computation.14 | loop fusion | bytes 16777216 | tf_op jit(solution)/shard_map/squeeze | solution.py:84
  253.5 40.1 %all-to-all-done = bf16[1,8,32,16,256]{4,3,1,0,2:T(8,128)(2,1)S(1)} async-done(((bf16[1,8,32,16,256]{4,3,1,0,2:T(8,128)(2,1)}), bf16[1,8,32,16,256]{4,3,1,0,2:T(8,128)(2,1)S(1)}, u32[]{:S(2)}, u32[]{:S(2)}) %all-to-all-start) | async-done | bytes 2097184 | tf_op jit(solution)/shard_map/all_to_all | solution.py:81
  293.6 8.0 %fusion.34 = f32[8,16,1024]{2,1,0:T(8,128)S(1)} fusion(bf16[32,128,512]{2,1,0:T(8,128)(2,1)} %get-tuple-element.12, bf16[32,128,512]{2,1,0:T(8,128)(2,1)} %fusion.73, bf16[32,128,512]{2,1,0:T(8,128)(2,1)} %get-tuple-element.11, bf16[1,8,32,16,256]{4,3,1,0,2:T(8,128)(2,1)S(1)} %all-to-all-done), kind=kOutput, calls=%fused_computation.76 | convolution fusion | flops 2214592512 | bytes 15204352 | tf_op jit(solution)/shard_map/jrk,jkx->rx/dot_general | solution.py:85
  301.6 13.6 %all_to_all.20 = f32[8,16,1024]{2,1,0:T(8,128)S(1)} all-to-all(f32[8,16,1024]{2,1,0:T(8,128)S(1)} %fusion.34), channel_id=1, replica_groups=mesh['pulse'=8,'tile'=32] {'pulse'}, dimensions={0} | all-to-all | bytes 1048576 | tf_op jit(solution)/shard_map/all_to_all | solution.py:22
  (57 shorter events, 7.2 us)
Async XLA Ops:
  6.5 237.0 %all-gather.2.cloned.1.call-start = ((), (), s32[]{:S(2)}) async-start(), calls=%async_computation.2 | async-start | bytes 8650752 | tf_op jit(solution)/shard_map/all_gather | solution.py:83
  8.1 5.8 %copy-start.3 = (s32[3,2,128]{2,1,0:T(2,128)S(1)}, s32[3,2,128]{2,1,0:T(2,128)}, u32[]{:S(2)}) copy-start(s32[3,2,128]{2,1,0:T(2,128)} %param.10) | copy-start | bytes 9220
  8.1 5.9 %copy-start.1 = (bf16[3,256,256]{2,1,0:T(8,128)(2,1)S(1)}, bf16[3,256,256]{2,1,0:T(8,128)(2,1)}, u32[]{:S(2)}) copy-start(bf16[3,256,256]{2,1,0:T(8,128)(2,1)} %param.8) | copy-start | bytes 1179652
  8.1 6.0 %copy-start.2 = (bf16[3,256,256]{2,1,0:T(8,128)(2,1)S(1)}, bf16[3,256,256]{2,1,0:T(8,128)(2,1)}, u32[]{:S(2)}) copy-start(bf16[3,256,256]{2,1,0:T(8,128)(2,1)} %param.9) | copy-start | bytes 1179652
  10.5 7.2 %collective-permute-start = (bf16[4096,256]{0,1:T(8,128)(2,1)S(1)}, bf16[4096,256]{0,1:T(8,128)(2,1)}, u32[]{:S(2)}, u32[]{:S(2)}) collective-permute-start(bf16[4096,256]{0,1:T(8,128)(2,1)S(1)} %fusion.9), channel_id=1, source_target_pairs={{0,1},{1,0},{2,3},{3,2},{4,5},{5,4},{6,7},{7,6},{8,9},{9,8},{10,11... | collective-permute-start | bytes 6291464 | tf_op jit(solution)/shard_map/ppermute | solution.py:12
  54.8 51.5 %collective-permute-start.1 = (bf16[4096,256]{0,1:T(8,128)(2,1)S(1)}, bf16[4096,256]{0,1:T(8,128)(2,1)}, u32[]{:S(2)}, u32[]{:S(2)}) collective-permute-start(bf16[4096,256]{0,1:T(8,128)(2,1)S(1)} %convolution_convert_fusion.2), channel_id=1, source_target_pairs={{0,2},{1,3},{2,0},{3,1},{4,6},{5,7},{6,4},{7,5},{8,10},{9,11},{10,... | collective-permute-start | bytes 6291464 | tf_op jit(solution)/shard_map/ppermute | solution.py:12
  143.3 54.5 %collective-permute-start.2 = (bf16[4096,256]{0,1:T(8,128)(2,1)S(1)}, bf16[4096,256]{0,1:T(8,128)(2,1)}, u32[]{:S(2)}, u32[]{:S(2)}) collective-permute-start(bf16[4096,256]{0,1:T(8,128)(2,1)S(1)} %convolution_convert_fusion.1), channel_id=1, source_target_pairs={{0,4},{1,5},{2,6},{3,7},{4,0},{5,1},{6,2},{7,3},{8,12},{9,13},{10,... | collective-permute-start | bytes 6291464 | tf_op jit(solution)/shard_map/ppermute | solution.py:12
  236.4 57.2 %all-to-all-start = ((bf16[1,8,32,16,256]{4,3,1,0,2:T(8,128)(2,1)}), bf16[1,8,32,16,256]{4,3,1,0,2:T(8,128)(2,1)S(1)}, u32[]{:S(2)}, u32[]{:S(2)}) async-start(bf16[1,8,32,16,256]{4,3,1,0,2:T(8,128)(2,1)} %copy.18), calls=%async_computation | async-start | bytes 4194304 | tf_op jit(solution)/shard_map/all_to_all | solution.py:81
  243.6 6.2 %copy-start = (bf16[1,32,2,128,512]{4,3,1,2,0:T(8,128)(2,1)S(1)}, bf16[1,32,2,128,512]{4,3,1,2,0:T(8,128)(2,1)}, u32[]{:S(2)}) copy-start(bf16[1,32,2,128,512]{4,3,1,2,0:T(8,128)(2,1)} %all-gather.2.cloned.1.call-done) | copy-start | bytes 25165828
Sparse Core Ops, SparseCore 0:
  56.4 108.3 all-gather.1
where the time goes:
time: 324 us; the launch traced here: 323 us
  waiting for transfers between devices  148 us (46%)
  other arithmetic  112 us (35%)
  matrix products  15.2 us (5%)
  between operations  13.8 us (4%)
  blocking collectives  13.6 us (4%)
  starting transfers between devices  12.2 us (4%)
  local copies, waits for them, and re-layouts  8.86 us (3%)
    ppermute x3, waiting for transfers between devices, partner_2(): return lax.ppermute(value, axis, pairs)  107 us
    select_n x6, other arithmetic, shift_rows(): result = jnp.where(doubled[None, :] == offset, window, result)  99.4 us
    all_to_all x1, waiting for transfers between devices, body(): lax.all_to_all(arranged, 'tile', split_axis=2, concat_axis=0, tiled=True)  40.1 us
    all_to_all x1, blocking collectives, summed_on_arrival(): lax.all_to_all(in_blocks(array, dim, length), axis, 0, 0, tiled=True)  13.6 us
    dot_general x1, matrix products, body(): jnp.einsum('jrk,jkx->rx', received, blocks, preferred_element_type=jnp.fl...  8.04 us
    all_to_all x1, starting transfers between devices, body(): lax.all_to_all(arranged, 'tile', split_axis=2, concat_axis=0, tiled=True)  7.11 us
  transfers between devices with their start and end apart: 5, of which 4 were waited for; matrix products, arithmetic and copies ran while one was open for 26% of the time, Pallas kernels for 0%

commit v1 on v0

v1 whole, which is shorter than its diff:
```python
import functools

import jax
import jax.numpy as jnp
from jax import lax
from jax.experimental import pallas as pl
from jax.experimental.pallas import tpu as pltpu
from jax.sharding import PartitionSpec as P

MESH = pl.DeviceIdType.MESH
F32 = jnp.float32
BF16 = jnp.bfloat16
HALO = 32
CHUNK = 256
WIDTH = 256
STREAMS = (("x", 0), ("y", 512), ("x", 256), ("y", 768))


def complex_block(real_part, imag_part):
    upper_half = jnp.concatenate([real_part, imag_part], axis=1)
    lower_half = jnp.concatenate([-imag_part, real_part], axis=1)
    return jnp.concatenate([upper_half, lower_half], axis=0)


def shifted(rows, table):
    groups = rows.shape[0] // 8
    at = lax.broadcasted_iota(jnp.int32, (8, 128), 0) + table
    index = jnp.bitwise_and(at + 8, 7)
    below, above = at < 0, at > 7
    picked = [
        jnp.take_along_axis(rows[8 * g : 8 * g + 8], index, axis=0, mode="promise_in_bounds")
        for g in range(groups)
    ]
    return jnp.concatenate(
        [
            jnp.where(below, picked[g - 1], jnp.where(above, picked[g + 1], picked[g]))
            for g in range(1, groups - 1)
        ],
        axis=0,
    )


def front_kernel(place, own_t, own_m, own_b, oth_t, oth_m, oth_b, re_ref, im_ref, table_ref, out_ref, w0, w1, buf0, buf1, buf2):
    g = pl.program_id(0)
    core, y_hi, z_lo = place[0], place[1], place[2]
    other = 1 - core

    @pl.when(g == 0)
    def _():
        for side, u in ((0, core), (1, other)):
            for h in range(2):
                a = re_ref[0, pl.ds(pl.multiple_of(u * 128, 128), 128), h * 128 : h * 128 + 128]
                b = im_ref[0, pl.ds(pl.multiple_of(u * 128, 128), 128), h * 128 : h * 128 + 128]
                r, c = side * 256, h * 256
                w0[r : r + 128, c : c + 128] = a
                w0[r : r + 128, c + 128 : c + 256] = b
                w0[r + 128 : r + 256, c : c + 128] = -b
                w0[r + 128 : r + 256, c + 128 : c + 256] = a
        for h in range(2):
            a = re_ref[1, pl.ds(pl.multiple_of(y_hi * 128, 128), 128), h * 128 : h * 128 + 128]
            b = im_ref[1, pl.ds(pl.multiple_of(y_hi * 128, 128), 128), h * 128 : h * 128 + 128]
            c = h * 256
            w1[0:128, c : c + 128] = a
            w1[0:128, c + 128 : c + 256] = b
            w1[128:256, c : c + 128] = -b
            w1[128:256, c + 128 : c + 256] = a

    first = jnp.logical_and(g == 0, core == 0)
    last = jnp.logical_and(g == pl.num_programs(0) - 1, core == 1)
    keep_top = jnp.where(first, 0.0, 1.0).astype(F32)
    keep_bottom = jnp.where(last, 0.0, 1.0).astype(F32)
    for side, (t, m, b) in enumerate(((own_t, own_m, own_b), (oth_t, oth_m, oth_b))):
        cols = slice(side * 256, side * 256 + 256)
        buf0[0:HALO, cols] = t[0].astype(F32) * keep_top
        buf0[HALO : HALO + CHUNK, cols] = m[0].astype(F32)
        buf0[HALO + CHUNK :, cols] = b[0].astype(F32) * keep_bottom

    parts = []
    for side, u in ((0, core), (1, other)):
        table = table_ref[0, pl.ds(u, 1), :]
        for half in range(2):
            c = side * 256 + half * 128
            parts.append(shifted(buf0[8 : 16 + 288 + 8, c : c + 128], table).astype(BF16))
    merged = jnp.dot(jnp.concatenate(parts, axis=1), w0[...], preferred_element_type=F32).astype(BF16)
    buf1[0:16, :] = merged[0:16].astype(F32) * keep_top
    buf1[16:272, :] = merged[16:272].astype(F32)
    buf1[272:288, :] = merged[272:288].astype(F32) * keep_bottom

    table = table_ref[1, pl.ds(y_hi, 1), :]
    for s in range(2):
        part = jnp.concatenate(
            [shifted(buf1[:, s * 256 + 128 * k : s * 256 + 128 * k + 128], table).astype(BF16) for k in range(2)], axis=1
        )
        merged = jnp.dot(part, w1[...], preferred_element_type=F32).astype(BF16)
        cols = slice(s * 512, s * 512 + 512)
        buf2[0:8, cols] = merged[0:8].astype(F32) * keep_top
        buf2[8:264, cols] = merged[8:264].astype(F32)
        buf2[264:272, cols] = merged[264:272].astype(F32) * keep_bottom

    table = table_ref[2, pl.ds(z_lo, 1), :]
    for k in range(8):
        moved = shifted(buf2[:, 128 * k : 128 * k + 128], table).astype(BF16)
        out_ref[0, 0, :, :, :, 128 * k : 128 * k + 128] = moved.reshape(4, 2, 32, 128)


def front(place, own, oth, merge_re, merge_im, range_shift):
    main = own.reshape(16, 256, 256), oth.reshape(16, 256, 256)
    edge = own.reshape(128, 32, 256), oth.reshape(128, 32, 256)
    top = pl.BlockSpec((1, 32, 256), lambda g, s: (jnp.maximum(8 * (2 * g + s[0]) - 1, 0), 0, 0))
    mid = pl.BlockSpec((1, 256, 256), lambda g, s: (2 * g + s[0], 0, 0))
    bot = pl.BlockSpec((1, 32, 256), lambda g, s: (jnp.minimum(8 * (2 * g + s[0]) + 8, 127), 0, 0))
    whole = pl.BlockSpec(memory_space=pltpu.VMEM)
    return pl.pallas_call(
        front_kernel,
        grid_spec=pltpu.PrefetchScalarGridSpec(
            num_scalar_prefetch=1,
            grid=(8,),
            in_specs=[top, mid, bot, top, mid, bot, whole, whole, whole],
            out_specs=pl.BlockSpec((1, 1, 4, 2, 32, 1024), lambda g, s: (g // 4, g % 4, 0, 0, 0, 0)),
            scratch_shapes=[
                pltpu.VMEM((512, 512), BF16),
                pltpu.VMEM((256, 512), BF16),
                pltpu.VMEM((CHUNK + 2 * HALO, 512), F32),
                pltpu.VMEM((288, 512), F32),
                pltpu.VMEM((272, 1024), F32),
            ],
        ),
        out_shape=jax.ShapeDtypeStruct((2, 4, 4, 2, 32, 1024), BF16),
        cost_estimate=pl.CostEstimate(flops=2_600_000_000, bytes_accessed=9_000_000, transcendentals=0),
        name="front",
    )(place, edge[0], main[0], edge[0], edge[1], main[1], edge[1], merge_re, merge_im, range_shift)


def image_kernel(lhs, maps, out_ref, rhs, acc_x, acc_y, fin, s1, r1, s2, r2, s3, r3, ss1, rs1, ss2, rs2, ss3, rs3):
    pulse, tile = lax.axis_index("pulse"), lax.axis_index("tile")
    y_lo, x = pulse // 4, pulse % 4
    z, y_hi, core = tile // 4, (tile // 2) % 2, tile % 2
    y = 2 * y_hi + y_lo

    def along_x(step):
        return (4 * y_lo + (x + step) % 4, tile)

    def along_y(step):
        to = (y + step) % 4
        return (4 * (to % 2) + x, 4 * z + 2 * (to // 2) + core)

    def along_z(to, its_core):
        return (pulse, 4 * to + 2 * y_hi + its_core)

    def z_other(to, its_core):
        return jnp.logical_or(to != z, its_core != core)

    barrier = pltpu.get_barrier_semaphore()
    for step in (1, 3):
        pl.semaphore_signal(barrier, inc=1, device_id=along_x(step), device_id_type=MESH)
        pl.semaphore_signal(barrier, inc=1, device_id=along_y(step), device_id_type=MESH)
    for off in range(16):
        to, its_core = (z + off // 2) % 8, (core + off % 2) % 2
        if off:
            pl.semaphore_signal(barrier, inc=1, device_id=along_z(to, its_core), device_id_type=MESH)

    for t in range(4):
        re, im = maps[t, 0], maps[t, 1]
        rhs[t * 256 : t * 256 + 128, 0:512] = re
        rhs[t * 256 : t * 256 + 128, 512:1024] = im
        rhs[t * 256 + 128 : t * 256 + 256, 0:512] = -im
        rhs[t * 256 + 128 : t * 256 + 256, 512:1024] = re

    def image_half(n, dest, h):
        kind, col = STREAMS[n]
        if kind == "x":
            rows = lhs[h, dest].reshape(256, 1024)
        else:
            rows = lhs[dest % 2, 2 * h : 2 * h + 2, :, dest // 2].reshape(256, 1024)
        return jnp.dot(rows, rhs[:, col : col + WIDTH], preferred_element_type=F32)

    def total_half(n, dest, h):
        if STREAMS[n][0] == "x":
            return acc_x[n // 2, dest % 2, h, :, dest // 2].reshape(64, WIDTH)
        return acc_y[n // 2, dest // 2, dest % 2, h].reshape(64, WIDTH)

    def ring(n, phase):
        kind = STREAMS[n][0]
        use_x = (kind == "x") == (phase == 1)
        here, to = (x, along_x) if use_x else (y, along_y)
        half = image_half if phase == 1 else total_half
        send, recv, ssem, rsem = (s1, r1, ss1, rs1) if phase == 1 else (s2, r2, ss2, rs2)
        return here, to, half, send, recv, ssem, rsem

    SLOTS = ((2, 0, 1), (2, 1, 3), (1, 1, 1), (3, 0, 3), (1, 0, 1), (3, 1, 3))

    def copy(n, phase, slot):
        here, to, half, send, recv, ssem, rsem = ring(n, phase)
        return pltpu.make_async_remote_copy(
            src_ref=send.at[n, slot],
            dst_ref=recv.at[n, slot],
            send_sem=ssem.at[n, slot],
            recv_sem=rsem.at[n, slot],
            device_id=to(SLOTS[slot][2]),
            device_id_type=MESH,
        )

    def open_ring(n, phase, wait_barrier=False):
        here, to, half, send, recv, ssem, rsem = ring(n, phase)
        for slot in range(4):
            ahead, h, _ = SLOTS[slot]
            send[n, slot] = half(n, (here + ahead) % 4, h).astype(BF16)
            if slot == 0 and wait_barrier:
                pl.semaphore_wait(barrier, 19)
            copy(n, phase, slot).start()

    def relay_ring(n, phase):
        here, to, half, send, recv, ssem, rsem = ring(n, phase)
        for slot in (4, 5):
            ahead, h, _ = SLOTS[slot]
            mine = half(n, (here + ahead) % 4, h)
            copy(n, phase, slot - 4).wait_recv()
            send[n, slot] = (mine + recv[n, slot - 4].astype(F32)).astype(BF16)
            copy(n, phase, slot).start()

    def close_ring(n, phase):
        here, to, half, send, recv, ssem, rsem = ring(n, phase)
        for h, slots in ((0, (3, 4)), (1, (2, 5))):
            value = half(n, here, h)
            for slot in slots:
                copy(n, phase, slot).wait_recv()
                value = value + recv[n, slot].astype(F32)
            if phase == 2:
                fin[n, 2 * h : 2 * h + 2] = value.reshape(2, 32, WIDTH)
            elif STREAMS[n][0] == "x":
                acc_x[n // 2, h] = value.reshape(2, 2, 2, 32, WIDTH)
            else:
                acc_y[n // 2, h] = value.reshape(2, 2, 2, 32, WIDTH)

    def z_copy(n, i, c, to, its_core, src_z):
        return pltpu.make_async_remote_copy(
            src_ref=s3.at[n, i, c],
            dst_ref=r3.at[n, src_z],
            send_sem=ss3.at[n, i, c],
            recv_sem=rs3.at[n, src_z],
            device_id=along_z(to, its_core),
            device_id_type=MESH,
        )

    def open_z(n):
        for i in range(4):
            for c in range(2):
                s3[n, i, c] = fin[n, i, 16 * c : 16 * c + 16].astype(BF16)
        for i in range(4):
            for c in range(2):
                to = 4 * core + i

                @pl.when(z_other(to, c))
                def _():
                    z_copy(n, i, c, to, c, z).start()

                @pl.when(jnp.logical_not(z_other(to, c)))
                def _():
                    r3[n, z] = s3[n, i, c]

    def close_z(n):
        col = STREAMS[n][1]
        source_core = z // 4
        value = jnp.zeros((16, WIDTH), F32)
        for off in range(8):
            src = (z + off) % 8

            @pl.when(z_other(src, source_core))
            def _():
                z_copy(n, 0, 0, (z + 1) % 8, core, src).wait_recv()

        for src in range(8):
            value = value + r3[n, src].astype(F32)
        out_ref[:, col : col + WIDTH] = value

    open_ring(0, 1, True)
    open_ring(1, 1)
    relay_ring(0, 1)
    relay_ring(1, 1)
    open_ring(2, 1)
    open_ring(3, 1)
    close_ring(0, 1)
    open_ring(0, 2)
    close_ring(1, 1)
    open_ring(1, 2)
    relay_ring(0, 2)
    relay_ring(1, 2)
    relay_ring(2, 1)
    relay_ring(3, 1)
    close_ring(0, 2)
    open_z(0)
    close_ring(1, 2)
    open_z(1)
    close_ring(2, 1)
    open_ring(2, 2)
    close_ring(3, 1)
    open_ring(3, 2)
    relay_ring(2, 2)
    relay_ring(3, 2)
    close_ring(2, 2)
    open_z(2)
    close_ring(3, 2)
    open_z(3)
    for n in range(4):
        close_z(n)
    for n in range(4):
        for slot in range(6):
            copy(n, 1, slot).wait_send()
            copy(n, 2, slot).wait_send()
        for i in range(4):
            for c in range(2):
                to = 4 * core + i

                @pl.when(z_other(to, c))
                def _():
                    z_copy(n, i, c, to, c, z).wait_send()


def image_sum(lhs, maps):
    vmem = pl.BlockSpec(memory_space=pltpu.VMEM)
    dma = pltpu.SemaphoreType.DMA
    return pl.pallas_call(
        image_kernel,
        out_shape=jax.ShapeDtypeStruct((16, 1024), F32),
        in_specs=[vmem, vmem],
        out_specs=vmem,
        scratch_shapes=[
            pltpu.VMEM((1024, 1024), BF16),
            pltpu.VMEM((2, 2, 2, 2, 2, 32, WIDTH), F32),
            pltpu.VMEM((2, 2, 2, 2, 2, 32, WIDTH), F32),
            pltpu.VMEM((4, 4, 32, WIDTH), F32),
            pltpu.VMEM((4, 6, 256, WIDTH), BF16),
            pltpu.VMEM((4, 6, 256, WIDTH), BF16),
            pltpu.VMEM((4, 6, 64, WIDTH), BF16),
            pltpu.VMEM((4, 6, 64, WIDTH), BF16),
            pltpu.VMEM((4, 4, 2, 16, WIDTH), BF16),
            pltpu.VMEM((4, 8, 16, WIDTH), BF16),
            dma((4, 6)),
            dma((4, 6)),
            dma((4, 6)),
            dma((4, 6)),
            dma((4, 4, 2)),
            dma((4, 8)),
        ],
        compiler_params=pltpu.CompilerParams(
            collective_id=0, has_side_effects=True, vmem_limit_bytes=48 * 1024 * 1024
        ),
        cost_estimate=pl.CostEstimate(flops=4_300_000_000, bytes_accessed=6_000_000, transcendentals=0),
        name="image_sum",
    )(lhs, maps)


def swap(value, mask):
    return lax.ppermute(value, "tile", [(t, t ^ mask) for t in range(lax.axis_size("tile"))])


def body(pulses, steering, merge_re, merge_im, range_shift, image_map):
    tile = lax.axis_index("tile")
    core, y_hi, z_lo = tile % 2, (tile // 2) % 2, (tile // 4) % 2
    own_map = image_map.reshape(256, 512)
    oth_map = swap(own_map, 4)
    stack = jnp.concatenate([own_map, oth_map], axis=0)

    def weights(h):
        a = lax.dynamic_slice(merge_re[2], (z_lo * 128, h * 128), (128, 128))
        b = lax.dynamic_slice(merge_im[2], (z_lo * 128, h * 128), (128, 128))
        return complex_block(a, -b)

    fold = jnp.concatenate([weights(z_lo), weights(1 - z_lo)], axis=1)
    mine = jnp.dot(fold, stack, preferred_element_type=F32).astype(BF16)
    far = swap(mine, 2)
    pair = jnp.stack([mine, far])
    near = swap(pair, 1)
    both = jnp.stack([pair, near])
    both = jnp.where(core == 1, both[::-1], both)
    both = jnp.where(y_hi == 1, both[:, ::-1], both)
    maps = both.reshape(4, 2, 128, 512)

    rows = pulses.reshape(pulses.shape[0], -1)
    own = jnp.dot(rows, complex_block(steering[0], steering[1]), preferred_element_type=F32).astype(BF16)
    oth = swap(own, 1)
    place = jnp.stack([core, y_hi, z_lo]).astype(jnp.int32)
    lhs = front(place, own, oth, merge_re, merge_im, range_shift)
    return image_sum(lhs, maps)


def solution(mesh):
    placed = (
        P(None, None, ("pulse", "tile")),
        P(),
        P(),
        P(),
        P(),
        P("pulse", "tile", None, None, None),
    )
    return jax.shard_map(
        body, mesh=mesh, in_specs=placed, out_specs=P(("pulse", "tile"), None), check_vma=False
    )
```

time: 324 us -> 94.7 us (0.29)
  waiting for transfers between devices: 148 us -> 14.5 us
  other arithmetic: 112 us -> 3.07 us
  Pallas kernels: 0 us -> 56.5 us
  between operations: 13.8 us -> 0.11 us
  blocking collectives: 13.6 us -> 0 us
  matrix products: 15.2 us -> 2.72 us
  starting transfers between devices: 12.2 us -> 7 us
    select_n x9 -> x2, other arithmetic: 105 us -> 0.42 us  [the longest x1 0.21 us: body(): both = jnp.where(y_hi == 1, both[:, ::-1], both)]
    ppermute x3 -> x4, waiting for transfers between devices: 107 us -> 14.5 us  [swap(): lax.ppermute(value, 'tile', [(t, t ^ mask) for t in range(lax.axis_size('...]
    pallas_call x0 -> x2, Pallas kernels: none -> 56.5 us  [the longest x1 46.4 us: image_sum(): pl.pallas_call(image_kernel, out_shape=jax.ShapeDtypeStruct((16, 1024), F...]
    all_to_all x1 -> x0, waiting for transfers between devices: 40.1 us -> none  [body(): lax.all_to_all(arranged, 'tile', split_axis=2, concat_axis=0, tiled=True)]
    all_to_all x1 -> x0, blocking collectives: 13.6 us -> none  [summed_on_arrival(): lax.all_to_all(in_blocks(array, dim, length), axis, 0, 0, tiled=True)]
    dot_general x5 -> x2, matrix products: 15.2 us -> 2.72 us  [the longest x1 2.41 us: body(): jnp.dot(rows, complex_block(steering[0], steering[1]), preferred_element_...]
    all_to_all x1 -> x0, starting transfers between devices: 7.11 us -> none  [body(): lax.all_to_all(arranged, 'tile', split_axis=2, concat_axis=0, tiled=True)]
    neg x4 -> x1, other arithmetic: 5.59 us -> 0.76 us  [complex_block(): lower_half = jnp.concatenate([-imag_part, real_part], axis=1)]
  transfers between devices with their start and end apart: 5 -> 4, of which waited for: 4 -> 2; matrix products, arithmetic and copies ran while one was open for 26% -> 5% of each run, Pallas kernels for 0% -> 0%
where the time goes in v1:
time: 94.7 us; the launch traced here: 94.1 us
  Pallas kernels  56.5 us (60%)
  waiting for transfers between devices  14.5 us (15%)
  local copies, waits for them, and re-layouts  10.2 us (11%)
  starting transfers between devices  7 us (7%)
  other arithmetic  3.07 us (3%)
  matrix products  2.72 us (3%)
    pallas_call x1, Pallas kernels, image_sum(): pl.pallas_call(image_kernel, out_shape=jax.ShapeDtypeStruct((16, 1024), F...  46.4 us
    ppermute x4, waiting for transfers between devices, swap(): lax.ppermute(value, 'tile', [(t, t ^ mask) for t in range(lax.axis_size('...  14.5 us
    pallas_call x1, Pallas kernels, front(): pl.pallas_call(front_kernel, grid_spec=pltpu.PrefetchScalarGridSpec(num_s...  10.1 us
    ppermute x4, starting transfers between devices, swap(): lax.ppermute(value, 'tile', [(t, t ^ mask) for t in range(lax.axis_size('...  7 us
    ppermute x1, local copies, waits for them, and re-layouts, swap(): lax.ppermute(value, 'tile', [(t, t ^ mask) for t in range(lax.axis_size('...  4.13 us
    unnamed x5, local copies, waits for them, and re-layouts  2.82 us
    convert_element_type x1, local copies, waits for them, and re-layouts, body(): jnp.dot(rows, complex_block(steering[0], steering[1]), preferred_element_...  2.44 us
    dot_general x1, matrix products, body(): jnp.dot(rows, complex_block(steering[0], steering[1]), preferred_element_...  2.41 us
  transfers between devices with their start and end apart: 4, of which 2 were waited for; matrix products, arithmetic and copies ran while one was open for 5% of the time, Pallas kernels for 0%

profile of v1, /device:TPU:1, one launch (start us, length us, event | category | flops | bytes accessed | tf_op | source)
XLA Modules:
  0.0 94.1 jit_solution(13909950233968963974)
XLA Ops:
  0.0 0.8 slice_bitcast_fusion
  0.8 0.8 fusion.30
  1.6 0.0 slice-start.1
  1.6 2.4 %fusion = bf16[4096,256]{0,1:T(8,128)(2,1)S(1)} fusion(bf16[512,8,2,128]{3,2,1,0:T(2,128)(2,1)} %bitcast.43, bf16[128,128]{1,0:T(8,128)(2,1)S(1)} %get-tuple-element.16, bf16[128,128]{1,0:T(8,128)(2,1)S(1)} %fusion.30, bf16[128,128]{1,0:T(8,128)(2,1)S(1)} %get-tuple-element.15), kind=kOutput, calls=%fused_computation.1 | convolution fusion | flops 538443776 | bytes 4292608 | tf_op jit(solution)/shard_map/dot_general | solution.py:380
  4.0 3.3 %collective-permute-start = (bf16[4096,256]{0,1:T(8,128)(2,1)S(1)}, bf16[4096,256]{0,1:T(8,128)(2,1)}, u32[]{:S(2)}, u32[]{:S(2)}) collective-permute-start(bf16[4096,256]{0,1:T(8,128)(2,1)S(1)} %fusion), channel_id=1, source_target_pairs={{0,1},{1,0},{2,3},{3,2},{4,5},{5,4},{6,7},{7,6},{8,9},{9,8},{10,11... | collective-permute-start | bytes 6291464 | tf_op jit(solution)/shard_map/ppermute | solution.py:354
  7.3 0.0 collective-permute-start.1
  7.4 7.7 %collective-permute-done.1 = bf16[256,512]{1,0:T(8,128)(2,1)S(1)} collective-permute-done((bf16[256,512]{1,0:T(8,128)(2,1)S(1)}, bf16[256,512]{1,0:T(8,128)(2,1)S(1)}, u32[]{:S(2)}, u32[]{:S(2)}) %collective-permute-start.1) | collective-permute-done | bytes 262176 | tf_op jit(solution)/shard_map/ppermute | solution.py:354
  15.0 0.3 convolution_convert_fusion.1
  15.4 1.6 %collective-permute-start.2 = (bf16[256,512]{1,0:T(8,128)(2,1)S(1)}, bf16[256,512]{1,0:T(8,128)(2,1)S(1)}, u32[]{:S(2)}, u32[]{:S(2)}) collective-permute-start(bf16[256,512]{1,0:T(8,128)(2,1)S(1)} %convolution_convert_fusion.1), channel_id=1, source_target_pairs={{0,2},{1,3},{2,0},{3,1},{4,6},{5,7},{6,4},{7,5},{8,10},{9,11},{10,... | collective-permute-start | bytes 786440 | tf_op jit(solution)/shard_map/ppermute | solution.py:354
  17.0 6.9 %collective-permute-done.2 = bf16[256,512]{1,0:T(8,128)(2,1)S(1)} collective-permute-done((bf16[256,512]{1,0:T(8,128)(2,1)S(1)}, bf16[256,512]{1,0:T(8,128)(2,1)S(1)}, u32[]{:S(2)}, u32[]{:S(2)}) %collective-permute-start.2) | collective-permute-done | bytes 262176 | tf_op jit(solution)/shard_map/ppermute | solution.py:354
  23.8 0.1 fusion.31
  23.9 2.1 %collective-permute-start.3 = (bf16[2,256,512]{2,1,0:T(8,128)(2,1)S(1)}, bf16[2,256,512]{2,1,0:T(8,128)(2,1)}, u32[]{:S(2)}, u32[]{:S(2)}) collective-permute-start(bf16[2,256,512]{2,1,0:T(8,128)(2,1)S(1)} %get-tuple-element.10), channel_id=1, source_target_pairs={{0,1},{1,0},{2,3},{3,2},{4,5},{5,4},{6,7},{7,6},{8,9},{9,8},{10,11... | collective-permute-start | bytes 1572872 | tf_op jit(solution)/shard_map/ppermute | solution.py:354
  26.0 2.4 %copy.7 = bf16[4096,256]{1,0:T(8,128)(2,1)} copy(bf16[4096,256]{0,1:T(8,128)(2,1)S(1)} %fusion) | data formatting | bytes 4194304 | tf_op jit(solution)/shard_map/convert_element_type | solution.py:380
  28.4 0.6 pad_add_fusion.place
  29.1 0.0 collective-permute-done.3
  29.1 1.1 %pad_maximum_fusion = bf16[2,2,256,512]{3,2,1,0:T(8,128)(2,1)S(1)} fusion(bf16[1,2,256,512]{3,2,1,0:T(8,128)(2,1)} %bitcast.18, bf16[1,2,256,512]{3,2,1,0:T(8,128)(2,1)S(1)} %get-tuple-element.9), kind=kLoop, calls=%fused_computation.7 | loop fusion | flops 524288 | bytes 2097152 | tf_op jit(solution)/shard_map/stack | solution.py:374
  30.2 0.2 reverse_select_fusion.1
  30.4 0.2 reverse_select_fusion
  30.7 0.0 collective-permute-done
  30.7 4.1 %copy.9 = bf16[4096,256]{1,0:T(8,128)(2,1)} copy(bf16[4096,256]{0,1:T(8,128)(2,1)} %collective-permute-done) | data formatting | bytes 4194304 | tf_op jit(solution)/shard_map/ppermute | solution.py:354
  34.8 10.1 %front.1.lhs = bf16[2,4,4,2,32,1024]{5,4,3,2,1,0:T(8,128)(2,1)} custom-call(s32[3]{0:T(128)} %pad_add_fusion.place, bf16[128,32,256]{2,1,0:T(8,128)(2,1)} %bitcast.37, bf16[16,256,256]{2,1,0:T(8,128)(2,1)} %bitcast.39, bf16[128,32,256]{2,1,0:T(8,128)(2,1)} %bitcast.38, bf16[128,32,256]{2,1,0:T(8,128)(2,1)} %bitcast.40, bf16[16,256,256]{2,1,0:T(8,128)(2,1)} %bitcast.42, ...), custom_call_target="tpu_custom_call" | custom-call | flops 2600000000 | bytes 9000000 | tf_op jit(solution)/shard_map/front/pallas_call | solution.py:113
  44.9 2.2 %copy-done = bf16[2,4,4,2,32,1024]{5,4,3,2,1,0:T(8,128)(2,1)S(1)} copy-done((bf16[2,4,4,2,32,1024]{5,4,3,2,1,0:T(8,128)(2,1)S(1)}, bf16[2,4,4,2,32,1024]{5,4,3,2,1,0:T(8,128)(2,1)}, u32[]{:S(2)}) %copy-start) | copy-done | bytes 4194328
  47.1 46.4 %image_sum.1 = f32[16,1024]{1,0:T(8,128)S(1)} custom-call(bf16[2,4,4,2,32,1024]{5,4,3,2,1,0:T(8,128)(2,1)S(1)} %copy-done, bf16[4,2,128,512]{3,2,1,0:T(8,128)(2,1)S(1)} %bitcast.36), custom_call_target="tpu_custom_call" | custom-call | flops 4300000256 | bytes 6000000 | tf_op jit(solution)/shard_map/image_sum/pallas_call | solution.py:322
  93.5 0.6 copy.17
  (8 shorter events, 0.1 us)
Async XLA Ops:
  1.5 5.7 %copy-start.1 = (bf16[1,1,2,128,512]{4,3,2,1,0:T(8,128)(2,1)S(1)}, bf16[1,1,2,128,512]{4,3,2,1,0:T(8,128)(2,1)}, u32[]{:S(2)}) copy-start(bf16[1,1,2,128,512]{4,3,2,1,0:T(8,128)(2,1)} %param.11) | copy-start | bytes 786436
  1.5 5.7 %slice-start = ((bf16[3,256,256]{2,1,0:T(8,128)(2,1)}), bf16[1,256,256]{2,1,0:T(8,128)(2,1)S(1)}, s32[]{:S(2)}) async-start(bf16[3,256,256]{2,1,0:T(8,128)(2,1)} %re_ref.1), calls=%async_computation | async-start | bytes 262144 | tf_op jit(solution)/shard_map/slice | solution.py:365
  1.6 5.8 %slice-start.1 = ((bf16[3,256,256]{2,1,0:T(8,128)(2,1)}), bf16[1,256,256]{2,1,0:T(8,128)(2,1)S(1)}, s32[]{:S(2)}) async-start(bf16[3,256,256]{2,1,0:T(8,128)(2,1)} %im_ref.1), calls=%async_computation.1 | async-start | bytes 262144 | tf_op jit(solution)/shard_map/slice | solution.py:366
  4.0 26.7 %collective-permute-start = (bf16[4096,256]{0,1:T(8,128)(2,1)S(1)}, bf16[4096,256]{0,1:T(8,128)(2,1)}, u32[]{:S(2)}, u32[]{:S(2)}) collective-permute-start(bf16[4096,256]{0,1:T(8,128)(2,1)S(1)} %fusion), channel_id=1, source_target_pairs={{0,1},{1,0},{2,3},{3,2},{4,5},{5,4},{6,7},{7,6},{8,9},{9,8},{10,11... | collective-permute-start | bytes 6291464 | tf_op jit(solution)/shard_map/ppermute | solution.py:354
  7.3 7.8 %collective-permute-start.1 = (bf16[256,512]{1,0:T(8,128)(2,1)S(1)}, bf16[256,512]{1,0:T(8,128)(2,1)S(1)}, u32[]{:S(2)}, u32[]{:S(2)}) collective-permute-start(bf16[256,512]{1,0:T(8,128)(2,1)S(1)} %bitcast.46), channel_id=1, source_target_pairs={{0,4},{1,5},{2,6},{3,7},{4,0},{5,1},{6,2},{7,3},{8,12},{9,13},{10,... | collective-permute-start | bytes 786440 | tf_op jit(solution)/shard_map/ppermute | solution.py:354
  15.4 8.5 %collective-permute-start.2 = (bf16[256,512]{1,0:T(8,128)(2,1)S(1)}, bf16[256,512]{1,0:T(8,128)(2,1)S(1)}, u32[]{:S(2)}, u32[]{:S(2)}) collective-permute-start(bf16[256,512]{1,0:T(8,128)(2,1)S(1)} %convolution_convert_fusion.1), channel_id=1, source_target_pairs={{0,2},{1,3},{2,0},{3,1},{4,6},{5,7},{6,4},{7,5},{8,10},{9,11},{10,... | collective-permute-start | bytes 786440 | tf_op jit(solution)/shard_map/ppermute | solution.py:354
  23.9 5.2 %collective-permute-start.3 = (bf16[2,256,512]{2,1,0:T(8,128)(2,1)S(1)}, bf16[2,256,512]{2,1,0:T(8,128)(2,1)}, u32[]{:S(2)}, u32[]{:S(2)}) collective-permute-start(bf16[2,256,512]{2,1,0:T(8,128)(2,1)S(1)} %get-tuple-element.10), channel_id=1, source_target_pairs={{0,1},{1,0},{2,3},{3,2},{4,5},{5,4},{6,7},{7,6},{8,9},{9,8},{10,11... | collective-permute-start | bytes 1572872 | tf_op jit(solution)/shard_map/ppermute | solution.py:354
  44.9 2.2 %copy-start = (bf16[2,4,4,2,32,1024]{5,4,3,2,1,0:T(8,128)(2,1)S(1)}, bf16[2,4,4,2,32,1024]{5,4,3,2,1,0:T(8,128)(2,1)}, u32[]{:S(2)}) copy-start(bf16[2,4,4,2,32,1024]{5,4,3,2,1,0:T(8,128)(2,1)} %front.1.lhs) | copy-start | bytes 12582916

commit v2 on v0

v2 whole, which is shorter than its diff:
```python
import jax
import jax.numpy as jnp
from jax import lax
from jax.experimental import pallas as pl
from jax.experimental.pallas import tpu as pltpu
from jax.sharding import PartitionSpec as P

MESH = pl.DeviceIdType.MESH
F32 = jnp.float32
BF16 = jnp.bfloat16
WIDTH = 256
STREAMS = ("x", "y", "x", "y")
TOWARD = (1, 3, 1, 3, 1, 3)


def dot(a, b):
    return jnp.dot(a, b, preferred_element_type=F32)


def shifted(rows, table):
    groups = rows.shape[0] // 8
    at = lax.broadcasted_iota(jnp.int32, (8, 128), 0) + table
    index = jnp.bitwise_and(at + 8, 7)
    below, above = at < 0, at > 7
    picked = [
        jnp.take_along_axis(rows[8 * g : 8 * g + 8], index, axis=0, mode="promise_in_bounds")
        for g in range(groups)
    ]
    return jnp.concatenate(
        [
            jnp.where(below, picked[g - 1], jnp.where(above, picked[g + 1], picked[g]))
            for g in range(1, groups - 1)
        ],
        axis=0,
    )


def kernel(
    pulses, steer_in, re_in, im_in, table_in, map_in, out_ref,
    steer, re_ref, im_ref, table_ref, own_map, pbuf, ws, w0, w1, w2, qbuf, buf0, buf1, buf2, lhs, mbuf, nbuf, rhs, held, total,
    s1, r1, sa2, ra2, sb2, rb2, sa3, ra3, sb3, rb3, small,
    ins, po, ps, pr, ms, mr, ns, nr, ss1, rs1, ss2, rs2, ss3, rs3,
):
    pulse, tile = lax.axis_index("pulse"), lax.axis_index("tile")
    y_lo, x = pulse // 4, pulse % 4
    z, y_hi, core = tile // 4, (tile // 2) % 2, tile % 2
    y, z_lo, other = 2 * y_hi + y_lo, z % 2, 1 - core

    def along_x(step):
        return (4 * y_lo + (x + step) % 4, tile)

    def along_y(step):
        to = (y + step) % 4
        return (4 * (to % 2) + x, 4 * z + 2 * (to // 2) + core)

    def along_z(to, its_core):
        return (pulse, 4 * to + 2 * y_hi + its_core)

    def z_other(to, its_core):
        return jnp.logical_or(to != z, its_core != core)

    z_mate = along_z(z + 1 - 2 * z_lo, core)
    core_mate = along_z(z, other)
    y_mate = along_y(2)

    fetches = [
        pltpu.make_async_copy(src, dst, ins.at[i])
        for i, (src, dst) in enumerate(
            ((map_in, own_map), (steer_in, steer), (re_in, re_ref), (im_in, im_ref), (table_in, table_ref))
        )
    ]
    for fetch in fetches:
        fetch.start()

    barrier = pltpu.get_barrier_semaphore()
    for step in (1, 2, 3):
        pl.semaphore_signal(barrier, inc=1, device_id=along_x(step), device_id_type=MESH)
        pl.semaphore_signal(barrier, inc=1, device_id=along_y(step), device_id_type=MESH)
    for off in range(1, 16):
        mate = along_z((z + off // 2) % 8, (core + off % 2) % 2)
        pl.semaphore_signal(barrier, inc=1, device_id=mate, device_id_type=MESH)

    def rows_of(side, g, c):
        wanted = g * 1024 + c * 512 - 64
        start = jnp.clip(wanted, 0, pulses.shape[0] - 640)
        at = 64 + start - wanted
        return (
            pulses.at[pl.ds(pl.multiple_of(start, 64), 640)],
            pbuf.at[side, g, pl.ds(pl.multiple_of(at, 64), 640)],
        )

    def own_copy(g):
        src, dst = rows_of(0, g, core)
        return pltpu.make_async_copy(src, dst, po.at[g])

    def mate_copy(g):
        src, dst = rows_of(1, g, other)
        return pltpu.make_async_remote_copy(
            src_ref=src, dst_ref=dst, send_sem=ps.at[0], recv_sem=pr.at[g], device_id=core_mate, device_id_type=MESH
        )

    def drain(ref, sem):
        pltpu.make_async_copy(ref, ref, sem).wait()

    def order(k):
        ahead = jnp.where(k < 2, 2, jnp.where(k < 4, 1, jnp.where(k < 6, 3, 0)))
        return 4 * (k % 2) + (x + ahead) % 4

    @pl.loop(0, 8)
    def _(k):
        own_copy(order(k)).start()

    zeros = jnp.zeros((64, 128), BF16)

    @pl.when(core == 0)
    def _():
        pbuf[0, 0, 64:128] = zeros
        pbuf[1, 0, 64:128] = zeros

    @pl.when(core == 1)
    def _():
        pbuf[0, 7, 640:704] = zeros
        pbuf[1, 7, 640:704] = zeros

    def map_copy(q):
        return pltpu.make_async_remote_copy(
            src_ref=own_map.at[:, q * 128 : q * 128 + 128],
            dst_ref=mbuf.at[q],
            send_sem=ms.at[0],
            recv_sem=mr.at[q],
            device_id=z_mate,
            device_id_type=MESH,
        )

    fetches[0].wait()
    pl.semaphore_wait(barrier, 21)
    for q in range(4):
        map_copy(q).start()

    @pl.loop(0, 8)
    def _(k):
        mate_copy(order(k)).start()

    for fetch in fetches[1:]:
        fetch.wait()
    ws[:, 0:128] = steer[0]
    ws[:, 128:256] = steer[1]

    def weight(level, u, h):
        rows = pl.ds(pl.multiple_of(u * 128, 128), 128)
        cols = pl.ds(pl.multiple_of(h * 128, 128), 128)
        return re_ref[level, rows, cols], im_ref[level, rows, cols]

    for h in range(2):
        c = h * 256
        for side, u in ((0, core), (1, other)):
            r = side * 256
            a, b = weight(0, u, h)
            w0[r : r + 128, c : c + 128] = a
            w0[r : r + 128, c + 128 : c + 256] = b
            w0[r + 128 : r + 256, c : c + 128] = -b
            w0[r + 128 : r + 256, c + 128 : c + 256] = a
        a, b = weight(1, y_hi, h)
        w1[0:128, c : c + 128] = a
        w1[0:128, c + 128 : c + 256] = b
        w1[128:256, c : c + 128] = -b
        w1[128:256, c + 128 : c + 256] = a
    for i, h in ((0, z_lo), (1, 1 - z_lo)):
        a, b = weight(2, z_lo, h)
        c = i * 256
        w2[0:128, c : c + 128] = a
        w2[0:128, c + 128 : c + 256] = -b
        w2[128:256, c : c + 128] = b
        w2[128:256, c + 128 : c + 256] = a

    def chunk(k):
        g = order(k)
        first = jnp.logical_and(g == 0, core == 0)
        last = jnp.logical_and(g == 7, core == 1)
        keep_top = jnp.where(first, 0.0, 1.0).astype(F32)
        keep_bottom = jnp.where(last, 0.0, 1.0).astype(F32)
        own_copy(g).wait()
        drain(pbuf.at[1, g, 64:704], pr.at[g])
        for side in range(2):
            product = dot(pbuf[side, g, 64:704], ws[...])
            qbuf[side, 0], qbuf[side, 1] = product[:, 0:128], product[:, 128:256]
        for side in range(2):
            even, odd = pl.ds(0, 320, stride=2), pl.ds(1, 320, stride=2)
            c = side * 256
            buf0[:, c : c + 128] = (qbuf[side, 0, even, :] - qbuf[side, 1, odd, :]).astype(BF16).astype(F32)
            buf0[:, c + 128 : c + 256] = (qbuf[side, 1, even, :] + qbuf[side, 0, odd, :]).astype(BF16).astype(F32)
        parts = []
        for side, u in ((0, core), (1, other)):
            table = table_ref[0, pl.ds(u, 1), :]
            for part in range(2):
                c = side * 256 + part * 128
                parts.append(shifted(buf0[8:312, c : c + 128], table).astype(BF16))
        merged = dot(jnp.concatenate(parts, axis=1), w0[...]).astype(BF16)
        buf1[0:16, :] = merged[0:16].astype(F32) * keep_top
        buf1[16:272, :] = merged[16:272].astype(F32)
        buf1[272:288, :] = merged[272:288].astype(F32) * keep_bottom
        table = table_ref[1, pl.ds(y_hi, 1), :]
        for s in range(2):
            parts = [shifted(buf1[:, s * 256 + 128 * i : s * 256 + 128 * i + 128], table).astype(BF16) for i in range(2)]
            merged = dot(jnp.concatenate(parts, axis=1), w1[...]).astype(BF16)
            cols = slice(s * 512, s * 512 + 512)
            buf2[0:8, cols] = merged[0:8].astype(F32) * keep_top
            buf2[8:264, cols] = merged[8:264].astype(F32)
            buf2[264:272, cols] = merged[264:272].astype(F32) * keep_bottom
        table = table_ref[2, pl.ds(z_lo, 1), :]
        for i in range(8):
            moved = shifted(buf2[:, 128 * i : 128 * i + 128], table).astype(BF16)
            lhs[g // 4, g % 4, :, :, :, 128 * i : 128 * i + 128] = moved.reshape(4, 2, 32, 128)

    def chunks(start, stop):
        pl.loop(start, stop)(chunk)

    mine = 2 * core + y_hi

    def near_copy(q, kind):
        index = mine if kind < 2 else 2 * core + 1 - y_hi
        return pltpu.make_async_remote_copy(
            src_ref=nbuf.at[q, index],
            dst_ref=nbuf.at[q, index],
            send_sem=ns.at[0],
            recv_sem=nr.at[q, 0 if kind == 0 else 1],
            device_id=y_mate if kind == 0 else core_mate,
            device_id_type=MESH,
        )

    def fold_maps(q):
        map_copy(q).wait_recv()
        cols = slice(q * 128, q * 128 + 128)
        nbuf[q, mine] = (dot(w2[:, 0:256], own_map[:, cols]) + dot(w2[:, 256:512], mbuf[q])).astype(BF16)
        near_copy(q, 0).start()
        near_copy(q, 1).start()

    def forward_maps(q):
        near_copy(q, 0).wait_recv()
        near_copy(q, 2).start()

    def build_maps(q):
        drain(nbuf.at[q, 0:2], nr.at[q, 1])
        for t in range(4):
            re, im = nbuf[q, t, 0:128], nbuf[q, t, 128:256]
            rhs[q, t * 256 : t * 256 + 128, 0:128] = re
            rhs[q, t * 256 : t * 256 + 128, 128:256] = im
            rhs[q, t * 256 + 128 : t * 256 + 256, 0:128] = -im
            rhs[q, t * 256 + 128 : t * 256 + 256, 128:256] = re

    def image_block(n, dest):
        rows = lhs[:, dest] if STREAMS[n] == "x" else lhs[dest % 2, :, :, dest // 2]
        return dot(rows.reshape(512, 1024), rhs[n])

    def first(n):
        return (x, along_x) if STREAMS[n] == "x" else (y, along_y)

    LANES = (slice(0, 128), slice(128, 256))

    def ring_copy(n, slot, part):
        _, to = first(n)
        src, dst = (s1.at[n, slot], r1.at[n, slot]) if part is None else (s1.at[n, slot, part], r1.at[n, slot, part])
        return pltpu.make_async_remote_copy(
            src_ref=src,
            dst_ref=dst,
            send_sem=ss1.at[n],
            recv_sem=rs1.at[n, slot if slot < 2 else 3 if part == 1 else 2],
            device_id=to(TOWARD[slot]),
            device_id_type=MESH,
        )

    def parts_of(n):
        return (None,) if n < 2 else (0, 1)

    def send_far(n):
        here, _ = first(n)
        block = image_block(n, (here + 2) % 4).astype(BF16)
        for h in range(2):
            for part in range(2):
                s1[n, h, part] = block[256 * h : 256 * h + 256, LANES[part]]
            ring_copy(n, h, None).start()

    def send_near(n):
        here, _ = first(n)
        for slot, ahead, h in ((2, 1, 1), (3, 3, 0)):
            block = image_block(n, (here + ahead) % 4)
            mine = block[256 * h : 256 * h + 256].astype(BF16)
            for part in range(2):
                s1[n, slot, part] = mine[:, LANES[part]]
            for part in parts_of(n):
                ring_copy(n, slot, part).start()
            held[n, slot - 2] = block[256 - 256 * h : 512 - 256 * h]

    def take_own(n):
        here, _ = first(n)
        total[n] = image_block(n, here).reshape(2, 2, 2, 2, 32, WIDTH)

    def relay(n):
        for part in parts_of(n):
            for slot in (4, 5):
                if part != 1:
                    ring_copy(n, slot - 4, None).wait_recv()
                for p in (0, 1) if part is None else (part,):
                    value = held[n, slot - 4, :, LANES[p]] + r1[n, slot - 4, p].astype(F32)
                    s1[n, slot, p] = value.astype(BF16)
                ring_copy(n, slot, part).start()

    def gather(n, part):
        if part is None:
            drain(r1.at[n, 2:6], rs1.at[n, 2])
        else:
            drain(r1.at[n, 2:6, part], rs1.at[n, 2 + part])
        for p in (0, 1) if part is None else (part,):
            for h, slots in ((0, (3, 4)), (1, (2, 5))):
                value = total[n, h, :, :, :, :, LANES[p]].reshape(256, 128)
                for slot in slots:
                    value = value + r1[n, slot, p].astype(F32)
                total[n, h, :, :, :, :, LANES[p]] = value.reshape(2, 2, 2, 32, 128)

    def second(n):
        return (y, along_y) if STREAMS[n] == "x" else (x, along_x)

    def straight_copy(n, part, step):
        _, to = second(n)
        src, dst = (sb2.at[n, step - 1], rb2.at[n, step - 1]) if part is None else (
            sa2.at[n - 2, part, step - 1],
            ra2.at[n - 2, part, step - 1],
        )
        return pltpu.make_async_remote_copy(
            src_ref=src,
            dst_ref=dst,
            send_sem=ss2.at[n],
            recv_sem=rs2.at[n, part or 0],
            device_id=to(step),
            device_id_type=MESH,
        )

    def z_copy(n, part, to, its_core, at):
        src, dst = (sb3.at[n, at], rb3.at[n, z]) if part is None else (sa3.at[n - 2, 8 * part + at], ra3.at[n - 2, part, z])
        return pltpu.make_async_remote_copy(
            src_ref=src,
            dst_ref=dst,
            send_sem=ss3.at[n],
            recv_sem=rs3.at[n, part or 0],
            device_id=along_z(to, its_core),
            device_id_type=MESH,
        )

    keeps = core == z // 4

    def start_z(n, part):
        for i in range(4):
            for c in range(2):
                to = 4 * core + i

                @pl.when(z_other(to, c))
                def _():
                    z_copy(n, part, to, c, 2 * i + c).start()

                @pl.when(jnp.logical_not(z_other(to, c)))
                def _():
                    if part is None:
                        rb3[n, z] = sb3[n, 2 * i + c]
                    else:
                        ra3[n - 2, part, z] = sa3[n - 2, 8 * part + 2 * i + c]

    def await_z(n, part):
        got, sem = (rb3.at[n], rs3.at[n, 0]) if part is None else (ra3.at[n - 2, part], rs3.at[n, part])
        pl.when(keeps)(lambda: drain(got.at[0:7], sem))
        pl.when(jnp.logical_not(keeps))(lambda: drain(got, sem))

    def total_block(n, dest, part):
        lanes = LANES[part]
        if STREAMS[n] == "x":
            return total[n, dest % 2, :, :, dest // 2, :, lanes].reshape(128, 128)
        return total[n, dest // 2, dest % 2, :, :, :, lanes].reshape(128, 128)

    def send_straight(n, part):
        gather(n, part)
        here, _ = second(n)
        for step in (2, 1, 3):
            sa2[n - 2, part, step - 1] = total_block(n, (here + step) % 4, part).astype(BF16)
            straight_copy(n, part, step).start()

    def send_z(n, part):
        here, _ = second(n)
        value = total_block(n, here, part)
        drain(ra2.at[n - 2, part], rs2.at[n, part])
        for step in range(3):
            value = value + ra2[n - 2, part, step].astype(F32)
        sa3[n - 2, 8 * part : 8 * part + 8] = value.astype(BF16).reshape(8, 16, 128)
        start_z(n, part)

    def finish(n, part):
        await_z(n, part)
        value = jnp.zeros((16, 128), F32)
        for src in range(8):
            value = value + ra3[n - 2, part, src].astype(F32)
        out_ref[:, part * 512 + n * 128 : part * 512 + n * 128 + 128] = value

    def send_z_early(n):
        gather(n, None)
        for i in range(4):
            for c in range(2):
                rows = slice(16 * c, 16 * c + 16)
                for place in range(4):
                    if STREAMS[n] == "x":
                        block = total[n, place % 2, i // 2, i % 2, place // 2, rows]
                    else:
                        block = total[n, place // 2, place % 2, i // 2, i % 2, rows]
                    sb3[n, 2 * i + c, place] = block.astype(BF16)
        start_z(n, None)

    def send_straight_late(n):
        await_z(n, None)
        value = jnp.zeros((4, 16, WIDTH), F32)
        for src in range(8):
            value = value + rb3[n, src].astype(F32)
        small[n] = value
        here, _ = second(n)
        for step in (2, 1, 3):
            sb2[n, step - 1] = small[n, (here + step) % 4].astype(BF16)
            straight_copy(n, None, step).start()

    def finish_late(n):
        here, _ = second(n)
        value = small[n, here]
        drain(rb2.at[n], rs2.at[n, 0])
        for step in range(3):
            value = value + rb2[n, step].astype(F32)
        for part in range(2):
            out_ref[:, part * 512 + n * 128 : part * 512 + n * 128 + 128] = value[:, LANES[part]]

    def sent_z(n):
        full, some = (sb3.at[n], sb3.at[n, 0:7]) if n < 2 else (sa3.at[n - 2], sa3.at[n - 2, 0:14])
        pl.when(keeps)(lambda: drain(some, ss3.at[n]))
        pl.when(jnp.logical_not(keeps))(lambda: drain(full, ss3.at[n]))

    chunks(0, 3)
    fold_maps(0)
    chunks(3, 4)
    fold_maps(1)
    chunks(4, 6)
    fold_maps(2)
    chunks(6, 7)
    fold_maps(3)
    forward_maps(0)
    chunks(7, 8)
    build_maps(0)
    send_far(0)
    forward_maps(1)
    build_maps(1)
    send_far(1)
    send_near(0)
    forward_maps(2)
    send_near(1)
    forward_maps(3)
    build_maps(2)
    take_own(0)
    take_own(1)
    build_maps(3)
    relay(0)
    relay(1)
    send_far(2)
    send_far(3)
    send_near(2)
    send_z_early(0)
    send_near(3)
    send_z_early(1)
    take_own(2)
    take_own(3)
    relay(2)
    relay(3)
    drain(pulses.at[0:5120], ps.at[0])
    drain(own_map, ms.at[0])
    drain(nbuf.at[:, 0:3], ns.at[0])
    for n in range(2):
        drain(s1.at[n], ss1.at[n])
    send_straight(2, 0)
    send_straight(3, 0)
    send_straight(2, 1)
    send_straight(3, 1)
    send_straight_late(0)
    send_straight_late(1)
    send_z(2, 0)
    send_z(3, 0)
    send_z(2, 1)
    send_z(3, 1)
    finish_late(0)
    finish_late(1)
    for n in range(2):
        drain(s1.at[n + 2], ss1.at[n + 2])
        drain(sb2.at[n], ss2.at[n])
        drain(sa2.at[n], ss2.at[n + 2])
        sent_z(n)
    finish(2, 0)
    finish(3, 0)
    finish(2, 1)
    finish(3, 1)
    sent_z(2)
    sent_z(3)


def body(pulses, steering, merge_re, merge_im, range_shift, image_map):
    vmem = pl.BlockSpec(memory_space=pltpu.VMEM)
    dma = pltpu.SemaphoreType.DMA
    return pl.pallas_call(
        kernel,
        out_shape=jax.ShapeDtypeStruct((16, 1024), F32),
        in_specs=[pl.BlockSpec(memory_space=pltpu.HBM)] * 6,
        out_specs=vmem,
        scratch_shapes=[
            pltpu.VMEM((2, 128, 128), BF16),
            pltpu.VMEM((3, 256, 256), BF16),
            pltpu.VMEM((3, 256, 256), BF16),
            pltpu.VMEM((3, 2, 128), jnp.int32),
            pltpu.VMEM((256, 512), BF16),
            pltpu.VMEM((2, 8, 768, 128), BF16),
            pltpu.VMEM((128, 256), BF16),
            pltpu.VMEM((512, 512), BF16),
            pltpu.VMEM((256, 512), BF16),
            pltpu.VMEM((256, 512), BF16),
            pltpu.VMEM((2, 2, 640, 128), F32),
            pltpu.VMEM((320, 512), F32),
            pltpu.VMEM((288, 512), F32),
            pltpu.VMEM((272, 1024), F32),
            pltpu.VMEM((2, 4, 4, 2, 32, 1024), BF16),
            pltpu.VMEM((4, 256, 128), BF16),
            pltpu.VMEM((4, 4, 256, 128), BF16),
            pltpu.VMEM((4, 1024, WIDTH), BF16),
            pltpu.VMEM((4, 2, 256, WIDTH), F32),
            pltpu.VMEM((4, 2, 2, 2, 2, 32, WIDTH), F32),
            pltpu.VMEM((4, 6, 2, 256, 128), BF16),
            pltpu.VMEM((4, 6, 2, 256, 128), BF16),
            pltpu.VMEM((2, 2, 3, 128, 128), BF16),
            pltpu.VMEM((2, 2, 3, 128, 128), BF16),
            pltpu.VMEM((2, 3, 16, WIDTH), BF16),
            pltpu.VMEM((2, 3, 16, WIDTH), BF16),
            pltpu.VMEM((2, 16, 16, 128), BF16),
            pltpu.VMEM((2, 2, 8, 16, 128), BF16),
            pltpu.VMEM((2, 8, 4, 16, WIDTH), BF16),
            pltpu.VMEM((2, 8, 4, 16, WIDTH), BF16),
            pltpu.VMEM((2, 4, 16, WIDTH), F32),
            dma((5,)),
            dma((8,)),
            dma((1,)),
            dma((8,)),
            dma((1,)),
            dma((4,)),
            dma((1,)),
            dma((4, 2)),
            dma((4,)),
            dma((4, 4)),
            dma((4,)),
            dma((4, 2)),
            dma((4,)),
            dma((4, 2)),
        ],
        compiler_params=pltpu.CompilerParams(
            collective_id=0, has_side_effects=True, vmem_limit_bytes=66_000_000
        ),
        cost_estimate=pl.CostEstimate(flops=8_000_000_000, bytes_accessed=6_000_000, transcendentals=0),
        name="window",
    )(
        pulses.reshape(-1, pulses.shape[2]),
        steering,
        merge_re,
        merge_im,
        range_shift,
        image_map.reshape(256, 512),
    )


def solution(mesh):
    placed = (
        P(None, None, ("pulse", "tile")),
        P(),
        P(),
        P(),
        P(),
        P("pulse", "tile", None, None, None),
    )
    return jax.shard_map(
        body, mesh=mesh, in_specs=placed, out_specs=P(("pulse", "tile"), None), check_vma=False
    )
```

time: 324 us -> 55.4 us (0.17)
  waiting for transfers between devices: 148 us -> 0 us
  other arithmetic: 112 us -> 0 us
  Pallas kernels: 0 us -> 53.8 us
  matrix products: 15.2 us -> 0 us
  between operations: 13.8 us -> 0.01 us
  blocking collectives: 13.6 us -> 0 us
  starting transfers between devices: 12.2 us -> 0 us
  local copies, waits for them, and re-layouts: 8.86 us -> 1.47 us
    ppermute x3 -> x0, waiting for transfers between devices: 107 us -> none  [partner_2(): return lax.ppermute(value, axis, pairs)]
    select_n x9 -> x0, other arithmetic: 105 us -> none  [the longest x6 99.4 us: shift_rows(): result = jnp.where(doubled[None, :] == offset, window, result)]
    pallas_call x0 -> x1, Pallas kernels: none -> 53.8 us  [body(): pl.pallas_call(kernel, out_shape=jax.ShapeDtypeStruct((16, 1024), F32), i...]
    all_to_all x1 -> x0, waiting for transfers between devices: 40.1 us -> none  [body(): lax.all_to_all(arranged, 'tile', split_axis=2, concat_axis=0, tiled=True)]
    dot_general x5 -> x0, matrix products: 15.2 us -> none  [the longest x1 8.04 us: body(): jnp.einsum('jrk,jkx->rx', received, blocks, preferred_element_type=jnp.fl...]
    all_to_all x1 -> x0, blocking collectives: 13.6 us -> none  [summed_on_arrival(): lax.all_to_all(in_blocks(array, dim, length), axis, 0, 0, tiled=True)]
    all_to_all x1 -> x0, starting transfers between devices: 7.11 us -> none  [body(): lax.all_to_all(arranged, 'tile', split_axis=2, concat_axis=0, tiled=True)]
    neg x4 -> x0, other arithmetic: 5.59 us -> none  [complex_block(): lower_half = jnp.concatenate([-imag_part, real_part], axis=1)]
  transfers between devices with their start and end apart: 5 -> 0, of which waited for: 4 -> 0; matrix products, arithmetic and copies ran while one was open for 26% -> 0% of each run, Pallas kernels for 0% -> 0%
where the time goes in v2:
time: 55.4 us; the launch traced here: 55.3 us
  Pallas kernels  53.8 us (97%)
  local copies, waits for them, and re-layouts  1.47 us (3%)
    pallas_call x1, Pallas kernels, body(): pl.pallas_call(kernel, out_shape=jax.ShapeDtypeStruct((16, 1024), F32), i...  53.8 us
    unnamed x1, local copies, waits for them, and re-layouts  1.47 us

profile of v2, /device:TPU:1, one launch (start us, length us, event | category | flops | bytes accessed | tf_op | source)
XLA Modules:
  0.0 55.3 jit_solution(8421094854019472013)
XLA Ops:
  0.0 53.8 %window.1 = f32[16,1024]{1,0:T(8,128)} custom-call(bf16[8192,128]{1,0:T(8,128)(2,1)} %bitcast.2, bf16[2,128,128]{2,1,0:T(8,128)(2,1)} %steer_in.1, bf16[3,256,256]{2,1,0:T(8,128)(2,1)} %re_in.1, bf16[3,256,256]{2,1,0:T(8,128)(2,1)} %im_in.1, s32[3,2,128]{2,1,0:T(2,128)} %table_in.1, bf16[256,512]{1,0:T(8,128)(2,1)} %bitcast.3), custom_call_target="tpu_custom_call" | custom-call | flops 8000000000 | bytes 6000000 | tf_op jit(solution)/shard_map/window/pallas_call | solution.py:507
  53.8 1.5 %copy.8 = f32[16,1024]{1,0:T(8,128)} copy(f32[16,1024]{1,0:T(8,128)} %window.1) | data formatting | bytes 131072

commit v3 on v2

--- a/solution.py
+++ b/solution.py
@@ -11,6 +11,7 @@
 WIDTH = 256
 STREAMS = ("x", "y", "x", "y")
 TOWARD = (1, 3, 1, 3, 1, 3)
+Z_FIRST = ((0, 0), (0, 1), (1, 0), (1, 1))
 
 
 def dot(a, b):
@@ -37,9 +38,9 @@
 
 def kernel(
     pulses, steer_in, re_in, im_in, table_in, map_in, out_ref,
-    steer, re_ref, im_ref, table_ref, own_map, pbuf, ws, w0, w1, w2, qbuf, buf0, buf1, buf2, lhs, mbuf, nbuf, rhs, held, total,
+    steer, re_ref, im_ref, table_ref, own_map, pbuf, ws, w0, w1, w2, qbuf, buf0, buf1, buf2, lhs, mbuf, mfar, nbuf, rhs, held, total,
     s1, r1, sa2, ra2, sb2, rb2, sa3, ra3, sb3, rb3, small,
-    ins, po, ps, pr, ms, mr, ns, nr, ss1, rs1, ss2, rs2, ss3, rs3,
+    ins, po, ps, pr, ms, mr, ns, nr, ss1, rs1, ss2, rs2, ss3, rs3, chain,
 ):
     pulse, tile = lax.axis_index("pulse"), lax.axis_index("tile")
     y_lo, x = pulse // 4, pulse % 4
@@ -76,9 +77,20 @@
     for step in (1, 2, 3):
         pl.semaphore_signal(barrier, inc=1, device_id=along_x(step), device_id_type=MESH)
         pl.semaphore_signal(barrier, inc=1, device_id=along_y(step), device_id_type=MESH)
-    for off in range(1, 16):
-        mate = along_z((z + off // 2) % 8, (core + off % 2) % 2)
+    corner = (y_mate[0], 4 * (z + 1 - 2 * z_lo) + 2 * (1 - y_hi) + core)
+    near = (core_mate, corner, along_z((z + 1) % 8, core), along_z((z + 7) % 8, core))
+    for mate in near:
         pl.semaphore_signal(barrier, inc=1, device_id=mate, device_id_type=MESH)
+
+    def widen(k):
+        if k:
+            pl.semaphore_wait(chain.at[k - 1], 2)
+        for step in (1, 7):
+            pl.semaphore_signal(chain.at[k], inc=1, device_id=along_z((z + step) % 8, core), device_id_type=MESH)
+
+    def share_reach():
+        pl.semaphore_wait(chain.at[2], 2)
+        pl.semaphore_signal(chain.at[3], inc=1, device_id=core_mate, device_id_type=MESH)
 
     def rows_of(side, g, c):
         wanted = g * 1024 + c * 512 - 64
@@ -122,20 +134,24 @@
         pbuf[0, 7, 640:704] = zeros
         pbuf[1, 7, 640:704] = zeros
 
-    def map_copy(q):
+    def map_copy(q, kind):
         return pltpu.make_async_remote_copy(
             src_ref=own_map.at[:, q * 128 : q * 128 + 128],
-            dst_ref=mbuf.at[q],
-            send_sem=ms.at[0],
-            recv_sem=mr.at[q],
-            device_id=z_mate,
+            dst_ref=mbuf.at[q] if kind == 0 else mfar.at[q, kind - 1],
+            send_sem=ms.at[0 if kind == 0 else 1],
+            recv_sem=mr.at[q, kind],
+            device_id=(z_mate, y_mate, corner)[kind],
             device_id_type=MESH,
         )
 
     fetches[0].wait()
-    pl.semaphore_wait(barrier, 21)
-    for q in range(4):
-        map_copy(q).start()
+    pl.semaphore_wait(barrier, 10)
+    widen(0)
+    for q in range(2):
+        for kind in (2, 1, 0):
+            map_copy(q, kind).start()
+    for q in range(2, 4):
+        map_copy(q, 0).start()
 
     @pl.loop(0, 8)
     def _(k):
@@ -222,17 +238,23 @@
         return pltpu.make_async_remote_copy(
             src_ref=nbuf.at[q, index],
             dst_ref=nbuf.at[q, index],
-            send_sem=ns.at[0],
+            send_sem=ns.at[q // 2],
             recv_sem=nr.at[q, 0 if kind == 0 else 1],
             device_id=y_mate if kind == 0 else core_mate,
             device_id_type=MESH,
         )
 
     def fold_maps(q):
-        map_copy(q).wait_recv()
         cols = slice(q * 128, q * 128 + 128)
+        for kind in range(3 if q < 2 else 1):
+            map_copy(q, kind).wait_recv()
         nbuf[q, mine] = (dot(w2[:, 0:256], own_map[:, cols]) + dot(w2[:, 256:512], mbuf[q])).astype(BF16)
-        near_copy(q, 0).start()
+        if q < 2:
+            there = dot(w2[:, 0:256], mfar[q, 0]) + dot(w2[:, 256:512], mfar[q, 1])
+            nbuf[q, 2 * core + 1 - y_hi] = there.astype(BF16)
+            near_copy(q, 2).start()
+        else:
+            near_copy(q, 0).start()
         near_copy(q, 1).start()
 
     def forward_maps(q):
@@ -257,6 +279,8 @@
 
     LANES = (slice(0, 128), slice(128, 256))
 
+    LANES = (slice(0, 128), slice(128, 256))
+
     def ring_copy(n, slot, part):
         _, to = first(n)
         src, dst = (s1.at[n, slot], r1.at[n, slot]) if part is None else (s1.at[n, slot, part], r1.at[n, slot, part])
@@ -264,13 +288,10 @@
             src_ref=src,
             dst_ref=dst,
             send_sem=ss1.at[n],
-            recv_sem=rs1.at[n, slot if slot < 2 else 3 if part == 1 else 2],
+            recv_sem=rs1.at[n, slot if part is None else 2 + part],
             device_id=to(TOWARD[slot]),
             device_id_type=MESH,
         )
-
-    def parts_of(n):
-        return (None,) if n < 2 else (0, 1)
 
     def send_far(n):
         here, _ = first(n)
@@ -284,10 +305,9 @@
         here, _ = first(n)
         for slot, ahead, h in ((2, 1, 1), (3, 3, 0)):
             block = image_block(n, (here + ahead) % 4)
-            mine = block[256 * h : 256 * h + 256].astype(BF16)
+            away = block[256 * h : 256 * h + 256].astype(BF16)
             for part in range(2):
-                s1[n, slot, part] = mine[:, LANES[part]]
-            for part in parts_of(n):
+                s1[n, slot, part] = away[:, LANES[part]]
                 ring_copy(n, slot, part).start()
             held[n, slot - 2] = block[256 - 256 * h : 512 - 256 * h]
 
@@ -296,52 +316,44 @@
         total[n] = image_block(n, here).reshape(2, 2, 2, 2, 32, WIDTH)
 
     def relay(n):
-        for part in parts_of(n):
+        for part in range(2):
             for slot in (4, 5):
-                if part != 1:
+                if part == 0:
                     ring_copy(n, slot - 4, None).wait_recv()
-                for p in (0, 1) if part is None else (part,):
-                    value = held[n, slot - 4, :, LANES[p]] + r1[n, slot - 4, p].astype(F32)
-                    s1[n, slot, p] = value.astype(BF16)
+                value = held[n, slot - 4, :, LANES[part]] + r1[n, slot - 4, part].astype(F32)
+                s1[n, slot, part] = value.astype(BF16)
                 ring_copy(n, slot, part).start()
 
     def gather(n, part):
-        if part is None:
-            drain(r1.at[n, 2:6], rs1.at[n, 2])
-        else:
-            drain(r1.at[n, 2:6, part], rs1.at[n, 2 + part])
-        for p in (0, 1) if part is None else (part,):
-            for h, slots in ((0, (3, 4)), (1, (2, 5))):
-                value = total[n, h, :, :, :, :, LANES[p]].reshape(256, 128)
-                for slot in slots:
-                    value = value + r1[n, slot, p].astype(F32)
-                total[n, h, :, :, :, :, LANES[p]] = value.reshape(2, 2, 2, 32, 128)
+        drain(r1.at[n, 2:6, part], rs1.at[n, 2 + part])
+        for h, slots in ((0, (3, 4)), (1, (2, 5))):
+            value = total[n, h, :, :, :, :, LANES[part]].reshape(256, 128)
+            for slot in slots:
+                value = value + r1[n, slot, part].astype(F32)
+            total[n, h, :, :, :, :, LANES[part]] = value.reshape(2, 2, 2, 32, 128)
 
     def second(n):
         return (y, along_y) if STREAMS[n] == "x" else (x, along_x)
 
     def straight_copy(n, part, step):
         _, to = second(n)
-        src, dst = (sb2.at[n, step - 1], rb2.at[n, step - 1]) if part is None else (
-            sa2.at[n - 2, part, step - 1],
-            ra2.at[n - 2, part, step - 1],
-        )
+        send, recv = (sb2, rb2) if (n, part) in Z_FIRST else (sa2, ra2)
         return pltpu.make_async_remote_copy(
-            src_ref=src,
-            dst_ref=dst,
-            send_sem=ss2.at[n],
-            recv_sem=rs2.at[n, part or 0],
+            src_ref=send.at[n, part, step - 1],
+            dst_ref=recv.at[n, part, step - 1],
+            send_sem=ss2.at[n, part],
+            recv_sem=rs2.at[n, part],
             device_id=to(step),
             device_id_type=MESH,
         )
 
     def z_copy(n, part, to, its_core, at):
-        src, dst = (sb3.at[n, at], rb3.at[n, z]) if part is None else (sa3.at[n - 2, 8 * part + at], ra3.at[n - 2, part, z])
+        send, recv = (sb3, rb3) if (n, part) in Z_FIRST else (sa3, ra3)
         return pltpu.make_async_remote_copy(
-            src_ref=src,
-            dst_ref=dst,
-            send_sem=ss3.at[n],
-            recv_sem=rs3.at[n, part or 0],
+            src_ref=send.at[n, part, at],
+            dst_ref=recv.at[n, part, z],
+            send_sem=ss3.at[n, part],
+            recv_sem=rs3.at[n, part],
             device_id=along_z(to, its_core),
             device_id_type=MESH,
         )
@@ -349,25 +361,22 @@
     keeps = core == z // 4
 
     def start_z(n, part):
+        send, recv = (sb3, rb3) if (n, part) in Z_FIRST else (sa3, ra3)
         for i in range(4):
             for c in range(2):
-                to = 4 * core + i
+                to, at = 4 * core + i, 2 * i + c
 
                 @pl.when(z_other(to, c))
                 def _():
-                    z_copy(n, part, to, c, 2 * i + c).start()
+                    z_copy(n, part, to, c, at).start()
 
                 @pl.when(jnp.logical_not(z_other(to, c)))
                 def _():
-                    if part is None:
-                        rb3[n, z] = sb3[n, 2 * i + c]
-                    else:
-                        ra3[n - 2, part, z] = sa3[n - 2, 8 * part + 2 * i + c]
-
-    def await_z(n, part):
-        got, sem = (rb3.at[n], rs3.at[n, 0]) if part is None else (ra3.at[n - 2, part], rs3.at[n, part])
-        pl.when(keeps)(lambda: drain(got.at[0:7], sem))
-        pl.when(jnp.logical_not(keeps))(lambda: drain(got, sem))
+                    recv[n, part, z] = send[n, part, at]
+
+    def drain_z(ref, sem):
+        pl.when(keeps)(lambda: drain(ref.at[0:7], sem))
+        pl.when(jnp.logical_not(keeps))(lambda: drain(ref, sem))
 
     def total_block(n, dest, part):
         lanes = LANES[part]
@@ -379,126 +388,133 @@
         gather(n, part)
         here, _ = second(n)
         for step in (2, 1, 3):
-            sa2[n - 2, part, step - 1] = total_block(n, (here + step) % 4, part).astype(BF16)
+            sa2[n, part, step - 1] = total_block(n, (here + step) % 4, part).astype(BF16)
             straight_copy(n, part, step).start()
 
     def send_z(n, part):
         here, _ = second(n)
         value = total_block(n, here, part)
-        drain(ra2.at[n - 2, part], rs2.at[n, part])
+        drain(ra2.at[n, part], rs2.at[n, part])
         for step in range(3):
-            value = value + ra2[n - 2, part, step].astype(F32)
-        sa3[n - 2, 8 * part : 8 * part + 8] = value.astype(BF16).reshape(8, 16, 128)
+            value = value + ra2[n, part, step].astype(F32)
+        sa3[n, part] = value.astype(BF16).reshape(8, 16, 128)
         start_z(n, part)
 
-    def finish(n, part):
-        await_z(n, part)
-        value = jnp.zeros((16, 128), F32)
-        for src in range(8):
-            value = value + ra3[n - 2, part, src].astype(F32)
-        out_ref[:, part * 512 + n * 128 : part * 512 + n * 128 + 128] = value
-
-    def send_z_early(n):
-        gather(n, None)
+    def send_z_early(n, part):
+        gather(n, part)
+        lanes = LANES[part]
         for i in range(4):
             for c in range(2):
                 rows = slice(16 * c, 16 * c + 16)
                 for place in range(4):
                     if STREAMS[n] == "x":
-                        block = total[n, place % 2, i // 2, i % 2, place // 2, rows]
+                        block = total[n, place % 2, i // 2, i % 2, place // 2, rows, lanes]
                     else:
-                        block = total[n, place // 2, place % 2, i // 2, i % 2, rows]
-                    sb3[n, 2 * i + c, place] = block.astype(BF16)
-        start_z(n, None)
-
-    def send_straight_late(n):
-        await_z(n, None)
-        value = jnp.zeros((4, 16, WIDTH), F32)
+                        block = total[n, place // 2, place % 2, i // 2, i % 2, rows, lanes]
+                    sb3[n, part, 2 * i + c, place] = block.astype(BF16)
+        start_z(n, part)
+
+    def send_straight_late(n, part):
+        drain_z(rb3.at[n, part], rs3.at[n, part])
+        value = jnp.zeros((4, 16, 128), F32)
         for src in range(8):
-            value = value + rb3[n, src].astype(F32)
-        small[n] = value
+            value = value + rb3[n, part, src].astype(F32)
+        small[n, part] = value
         here, _ = second(n)
         for step in (2, 1, 3):
-            sb2[n, step - 1] = small[n, (here + step) % 4].astype(BF16)
-            straight_copy(n, None, step).start()
-
-    def finish_late(n):
+            sb2[n, part, step - 1] = small[n, part, (here + step) % 4].astype(BF16)
+            straight_copy(n, part, step).start()
+
+    def finish(n, part):
         here, _ = second(n)
-        value = small[n, here]
-        drain(rb2.at[n], rs2.at[n, 0])
-        for step in range(3):
-            value = value + rb2[n, step].astype(F32)
-        for part in range(2):
-            out_ref[:, part * 512 + n * 128 : part * 512 + n * 128 + 128] = value[:, LANES[part]]
-
-    def sent_z(n):
-        full, some = (sb3.at[n], sb3.at[n, 0:7]) if n < 2 else (sa3.at[n - 2], sa3.at[n - 2, 0:14])
-        pl.when(keeps)(lambda: drain(some, ss3.at[n]))
-        pl.when(jnp.logical_not(keeps))(lambda: drain(full, ss3.at[n]))
-
-    chunks(0, 3)
+        if (n, part) in Z_FIRST:
+            value = small[n, part, here]
+            drain(rb2.at[n, part], rs2.at[n, part])
+            for step in range(3):
+                value = value + rb2[n, part, step].astype(F32)
+        else:
+            drain_z(ra3.at[n, part], rs3.at[n, part])
+            value = jnp.zeros((16, 128), F32)
+            for src in range(8):
+                value = value + ra3[n, part, src].astype(F32)
+        out_ref[:, part * 512 + n * 128 : part * 512 + n * 128 + 128] = value
+
+    def sent(n, part):
+        if (n, part) in Z_FIRST:
+            drain(sb2.at[n, part], ss2.at[n, part])
+            drain_z(sb3.at[n, part], ss3.at[n, part])
+        else:
+            drain(sa2.at[n, part], ss2.at[n, part])
+            drain_z(sa3.at[n, part], ss3.at[n, part])
+
+    chunks(0, 5)
     fold_maps(0)
-    chunks(3, 4)
-    fold_maps(1)
-    chunks(4, 6)
-    fold_maps(2)
-    chunks(6, 7)
-    fold_maps(3)
-    forward_maps(0)
-    chunks(7, 8)
+    chunks(5, 7)
     build_maps(0)
     send_far(0)
-    forward_maps(1)
+    fold_maps(1)
+    chunks(7, 8)
     build_maps(1)
+    fold_maps(2)
     send_far(1)
+    widen(1)
     send_near(0)
+    fold_maps(3)
+    send_near(1)
+    widen(2)
+    take_own(0)
+    relay(0)
+    take_own(1)
     forward_maps(2)
-    send_near(1)
+    relay(1)
+    share_reach()
+    build_maps(2)
+    send_far(2)
     forward_maps(3)
-    build_maps(2)
-    take_own(0)
-    take_own(1)
     build_maps(3)
-    relay(0)
-    relay(1)
-    send_far(2)
     send_far(3)
     send_near(2)
-    send_z_early(0)
+    pl.semaphore_wait(chain.at[3], 1)
+    send_z_early(0, 0)
+    send_z_early(0, 1)
     send_near(3)
-    send_z_early(1)
+    send_z_early(1, 0)
+    send_z_early(1, 1)
     take_own(2)
     take_own(3)
     relay(2)
     relay(3)
     drain(pulses.at[0:5120], ps.at[0])
     drain(own_map, ms.at[0])
-    drain(nbuf.at[:, 0:3], ns.at[0])
+    drain(own_map, ms.at[1])
+    drain(nbuf.at[0:2, 0:2], ns.at[0])
+    drain(nbuf.at[2:4, 0:3], ns.at[1])
     for n in range(2):
         drain(s1.at[n], ss1.at[n])
     send_straight(2, 0)
     send_straight(3, 0)
     send_straight(2, 1)
     send_straight(3, 1)
-    send_straight_late(0)
-    send_straight_late(1)
+    send_straight_late(0, 0)
+    send_straight_late(0, 1)
     send_z(2, 0)
     send_z(3, 0)
+    send_straight_late(1, 0)
+    send_straight_late(1, 1)
     send_z(2, 1)
     send_z(3, 1)
-    finish_late(0)
-    finish_late(1)
     for n in range(2):
         drain(s1.at[n + 2], ss1.at[n + 2])
-        drain(sb2.at[n], ss2.at[n])
-        drain(sa2.at[n], ss2.at[n + 2])
-        sent_z(n)
+        for part in range(2):
+            finish(n, part)
+            sent(n, part)
     finish(2, 0)
     finish(3, 0)
     finish(2, 1)
     finish(3, 1)
-    sent_z(2)
-    sent_z(3)
+    for n in range(2, 4):
+        for part in range(2):
+            sent(n, part)
 
 
 def body(pulses, steering, merge_re, merge_im, range_shift, image_map):
@@ -506,7 +522,7 @@
     dma = pltpu.SemaphoreType.DMA
     return pl.pallas_call(
         kernel,
-        out_shape=jax.ShapeDtypeStruct((16, 1024), F32),
+        out_shape=pltpu.VMEM((16, 1024), F32),
         in_specs=[pl.BlockSpec(memory_space=pltpu.HBM)] * 6,
         out_specs=vmem,
         scratch_shapes=[
@@ -526,35 +542,37 @@
             pltpu.VMEM((272, 1024), F32),
             pltpu.VMEM((2, 4, 4, 2, 32, 1024), BF16),
             pltpu.VMEM((4, 256, 128), BF16),
+            pltpu.VMEM((2, 2, 256, 128), BF16),
             pltpu.VMEM((4, 4, 256, 128), BF16),
             pltpu.VMEM((4, 1024, WIDTH), BF16),
             pltpu.VMEM((4, 2, 256, WIDTH), F32),
             pltpu.VMEM((4, 2, 2, 2, 2, 32, WIDTH), F32),
             pltpu.VMEM((4, 6, 2, 256, 128), BF16),
             pltpu.VMEM((4, 6, 2, 256, 128), BF16),
-            pltpu.VMEM((2, 2, 3, 128, 128), BF16),
-            pltpu.VMEM((2, 2, 3, 128, 128), BF16),
-            pltpu.VMEM((2, 3, 16, WIDTH), BF16),
-            pltpu.VMEM((2, 3, 16, WIDTH), BF16),
-            pltpu.VMEM((2, 16, 16, 128), BF16),
-            pltpu.VMEM((2, 2, 8, 16, 128), BF16),
-            pltpu.VMEM((2, 8, 4, 16, WIDTH), BF16),
-            pltpu.VMEM((2, 8, 4, 16, WIDTH), BF16),
-            pltpu.VMEM((2, 4, 16, WIDTH), F32),
+            pltpu.VMEM((4, 2, 3, 128, 128), BF16),
+            pltpu.VMEM((4, 2, 3, 128, 128), BF16),
+            pltpu.VMEM((4, 2, 3, 16, 128), BF16),
+            pltpu.VMEM((4, 2, 3, 16, 128), BF16),
+            pltpu.VMEM((4, 2, 8, 16, 128), BF16),
+            pltpu.VMEM((4, 2, 8, 16, 128), BF16),
+            pltpu.VMEM((4, 2, 8, 4, 16, 128), BF16),
+            pltpu.VMEM((4, 2, 8, 4, 16, 128), BF16),
+            pltpu.VMEM((4, 2, 4, 16, 128), F32),
             dma((5,)),
             dma((8,)),
             dma((1,)),
             dma((8,)),
-            dma((1,)),
-            dma((4,)),
-            dma((1,)),
+            dma((2,)),
+            dma((4, 3)),
+            dma((2,)),
             dma((4, 2)),
             dma((4,)),
             dma((4, 4)),
-            dma((4,)),
             dma((4, 2)),
-            dma((4,)),
             dma((4, 2)),
+            dma((4, 2)),
+            dma((4, 2)),
+            pltpu.SemaphoreType.REGULAR((4,)),
         ],
         compiler_params=pltpu.CompilerParams(
             collective_id=0, has_side_effects=True, vmem_limit_bytes=66_000_000

time: 55.4 us -> 54 us (0.975)
  local copies, waits for them, and re-layouts: 1.47 us -> 0.63 us
  Pallas kernels: 53.8 us -> 53.2 us
    unnamed x1, local copies, waits for them, and re-layouts: 1.47 us -> 0.63 us
    pallas_call x1, Pallas kernels: 53.8 us -> 53.2 us  [body(): pl.pallas_call(kernel, out_shape=pltpu.VMEM((16, 1024), F32), in_specs=[p...]
where the time goes in v3:
time: 54 us; the launch traced here: 53.9 us
  Pallas kernels  53.2 us (99%)
  local copies, waits for them, and re-layouts  0.63 us (1%)
    pallas_call x1, Pallas kernels, body(): pl.pallas_call(kernel, out_shape=pltpu.VMEM((16, 1024), F32), in_specs=[p...  53.2 us

profile of v3, /device:TPU:1, one launch (start us, length us, event | category | flops | bytes accessed | tf_op | source)
XLA Modules:
  0.0 53.9 jit_solution(4549747729948414933)
XLA Ops:
  0.0 53.2 %window.1 = f32[16,1024]{1,0:T(8,128)S(1)} custom-call(bf16[8192,128]{1,0:T(8,128)(2,1)} %bitcast.2, bf16[2,128,128]{2,1,0:T(8,128)(2,1)} %steer_in.1, bf16[3,256,256]{2,1,0:T(8,128)(2,1)} %re_in.1, bf16[3,256,256]{2,1,0:T(8,128)(2,1)} %im_in.1, s32[3,2,128]{2,1,0:T(2,128)} %table_in.1, bf16[256,512]{1,0:T(8,128)(2,1)} %bitcast.3), custom_call_target="tpu_custom_call" | custom-call | flops 8000000000 | bytes 6000000 | tf_op jit(solution)/shard_map/window/pallas_call | solution.py:523
  53.2 0.6 %copy.8 = f32[16,1024]{1,0:T(8,128)} copy(f32[16,1024]{1,0:T(8,128)S(1)} %window.1) | data formatting | bytes 131072

commit v4 on v3

--- a/solution.py
+++ b/solution.py
@@ -93,7 +93,7 @@
         pl.semaphore_signal(chain.at[3], inc=1, device_id=core_mate, device_id_type=MESH)
 
     def rows_of(side, g, c):
-        wanted = g * 1024 + c * 512 - 64
+        wanted = g * 1024 + (1 - c) * 512 - 64
         start = jnp.clip(wanted, 0, pulses.shape[0] - 640)
         at = 64 + start - wanted
         return (
@@ -124,12 +124,12 @@
 
     zeros = jnp.zeros((64, 128), BF16)
 
-    @pl.when(core == 0)
+    @pl.when(core == 1)
     def _():
         pbuf[0, 0, 64:128] = zeros
         pbuf[1, 0, 64:128] = zeros
 
-    @pl.when(core == 1)
+    @pl.when(core == 0)
     def _():
         pbuf[0, 7, 640:704] = zeros
         pbuf[1, 7, 640:704] = zeros
@@ -147,11 +147,11 @@
     fetches[0].wait()
     pl.semaphore_wait(barrier, 10)
     widen(0)
-    for q in range(2):
+    def send_map(q):
         for kind in (2, 1, 0):
             map_copy(q, kind).start()
-    for q in range(2, 4):
-        map_copy(q, 0).start()
+
+    send_map(0)
 
     @pl.loop(0, 8)
     def _(k):
@@ -191,8 +191,8 @@
 
     def chunk(k):
         g = order(k)
-        first = jnp.logical_and(g == 0, core == 0)
-        last = jnp.logical_and(g == 7, core == 1)
+        first = jnp.logical_and(g == 0, core == 1)
+        last = jnp.logical_and(g == 7, core == 0)
         keep_top = jnp.where(first, 0.0, 1.0).astype(F32)
         keep_bottom = jnp.where(last, 0.0, 1.0).astype(F32)
         own_copy(g).wait()
@@ -233,36 +233,28 @@
 
     mine = 2 * core + y_hi
 
-    def near_copy(q, kind):
-        index = mine if kind < 2 else 2 * core + 1 - y_hi
+    def near_copy(q):
+        pair = nbuf.at[q, pl.ds(2 * core, 2)]
         return pltpu.make_async_remote_copy(
-            src_ref=nbuf.at[q, index],
-            dst_ref=nbuf.at[q, index],
-            send_sem=ns.at[q // 2],
-            recv_sem=nr.at[q, 0 if kind == 0 else 1],
-            device_id=y_mate if kind == 0 else core_mate,
+            src_ref=pair,
+            dst_ref=pair,
+            send_sem=ns.at[0],
+            recv_sem=nr.at[q],
+            device_id=core_mate,
             device_id_type=MESH,
         )
 
     def fold_maps(q):
-        cols = slice(q * 128, q * 128 + 128)
-        for kind in range(3 if q < 2 else 1):
+        for kind in range(3):
             map_copy(q, kind).wait_recv()
-        nbuf[q, mine] = (dot(w2[:, 0:256], own_map[:, cols]) + dot(w2[:, 256:512], mbuf[q])).astype(BF16)
-        if q < 2:
-            there = dot(w2[:, 0:256], mfar[q, 0]) + dot(w2[:, 256:512], mfar[q, 1])
-            nbuf[q, 2 * core + 1 - y_hi] = there.astype(BF16)
-            near_copy(q, 2).start()
-        else:
-            near_copy(q, 0).start()
-        near_copy(q, 1).start()
-
-    def forward_maps(q):
-        near_copy(q, 0).wait_recv()
-        near_copy(q, 2).start()
+        here = own_map[:, q * 128 : q * 128 + 128], mbuf[q]
+        there = mfar[q, 0], mfar[q, 1]
+        for index, (a, b) in ((mine, here), (2 * core + 1 - y_hi, there)):
+            nbuf[q, index] = (dot(w2[:, 0:256], a) + dot(w2[:, 256:512], b)).astype(BF16)
+        near_copy(q).start()
 
     def build_maps(q):
-        drain(nbuf.at[q, 0:2], nr.at[q, 1])
+        near_copy(q).wait_recv()
         for t in range(4):
             re, im = nbuf[q, t, 0:128], nbuf[q, t, 128:256]
             rhs[q, t * 256 : t * 256 + 128, 0:128] = re
@@ -358,13 +350,13 @@
             device_id_type=MESH,
         )
 
-    keeps = core == z // 4
+    keeps = core == 1 - z // 4
 
     def start_z(n, part):
         send, recv = (sb3, rb3) if (n, part) in Z_FIRST else (sa3, ra3)
         for i in range(4):
             for c in range(2):
-                to, at = 4 * core + i, 2 * i + c
+                to, at = 4 * other + i, 2 * i + c
 
                 @pl.when(z_other(to, c))
                 def _():
@@ -447,7 +439,12 @@
             drain(sa2.at[n, part], ss2.at[n, part])
             drain_z(sa3.at[n, part], ss3.at[n, part])
 
-    chunks(0, 5)
+    chunks(0, 2)
+    send_map(1)
+    chunks(2, 4)
+    send_map(2)
+    chunks(4, 5)
+    send_map(3)
     fold_maps(0)
     chunks(5, 7)
     build_maps(0)
@@ -455,24 +452,22 @@
     fold_maps(1)
     chunks(7, 8)
     build_maps(1)
-    fold_maps(2)
     send_far(1)
     widen(1)
     send_near(0)
-    fold_maps(3)
+    fold_maps(2)
     send_near(1)
+    relay(0)
     widen(2)
-    take_own(0)
-    relay(0)
-    take_own(1)
-    forward_maps(2)
-    relay(1)
-    share_reach()
     build_maps(2)
     send_far(2)
-    forward_maps(3)
+    take_own(0)
+    fold_maps(3)
+    take_own(1)
+    relay(1)
     build_maps(3)
     send_far(3)
+    share_reach()
     send_near(2)
     pl.semaphore_wait(chain.at[3], 1)
     send_z_early(0, 0)
@@ -481,14 +476,13 @@
     send_z_early(1, 0)
     send_z_early(1, 1)
     take_own(2)
+    relay(2)
     take_own(3)
-    relay(2)
     relay(3)
     drain(pulses.at[0:5120], ps.at[0])
     drain(own_map, ms.at[0])
-    drain(own_map, ms.at[1])
-    drain(nbuf.at[0:2, 0:2], ns.at[0])
-    drain(nbuf.at[2:4, 0:3], ns.at[1])
+    drain(mfar, ms.at[1])
+    drain(nbuf.at[:, 0:2], ns.at[0])
     for n in range(2):
         drain(s1.at[n], ss1.at[n])
     send_straight(2, 0)
@@ -542,7 +536,7 @@
             pltpu.VMEM((272, 1024), F32),
             pltpu.VMEM((2, 4, 4, 2, 32, 1024), BF16),
             pltpu.VMEM((4, 256, 128), BF16),
-            pltpu.VMEM((2, 2, 256, 128), BF16),
+            pltpu.VMEM((4, 2, 256, 128), BF16),
             pltpu.VMEM((4, 4, 256, 128), BF16),
             pltpu.VMEM((4, 1024, WIDTH), BF16),
             pltpu.VMEM((4, 2, 256, WIDTH), F32),
@@ -564,8 +558,8 @@
             dma((8,)),
             dma((2,)),
             dma((4, 3)),
-            dma((2,)),
-            dma((4, 2)),
+            dma((1,)),
+            dma((4,)),
             dma((4,)),
             dma((4, 4)),
             dma((4, 2)),

time: 54 us -> 49.9 us (0.924)
  Pallas kernels: 53.2 us -> 49.1 us
    pallas_call x1, Pallas kernels: 53.2 us -> 49.1 us  [body(): pl.pallas_call(kernel, out_shape=pltpu.VMEM((16, 1024), F32), in_specs=[p...]
where the time goes in v4:
time: 49.9 us; the launch traced here: 49.8 us
  Pallas kernels  49.1 us (98%)
  local copies, waits for them, and re-layouts  0.63 us (1%)
    pallas_call x1, Pallas kernels, body(): pl.pallas_call(kernel, out_shape=pltpu.VMEM((16, 1024), F32), in_specs=[p...  49.1 us

profile of v4, /device:TPU:1, one launch (start us, length us, event | category | flops | bytes accessed | tf_op | source)
XLA Modules:
  0.0 49.8 jit_solution(7229648367222161745)
XLA Ops:
  0.0 49.1 %window.1 = f32[16,1024]{1,0:T(8,128)S(1)} custom-call(bf16[8192,128]{1,0:T(8,128)(2,1)} %bitcast.2, bf16[2,128,128]{2,1,0:T(8,128)(2,1)} %steer_in.1, bf16[3,256,256]{2,1,0:T(8,128)(2,1)} %re_in.1, bf16[3,256,256]{2,1,0:T(8,128)(2,1)} %im_in.1, s32[3,2,128]{2,1,0:T(2,128)} %table_in.1, bf16[256,512]{1,0:T(8,128)(2,1)} %bitcast.3), custom_call_target="tpu_custom_call" | custom-call | flops 8000000000 | bytes 6000000 | tf_op jit(solution)/shard_map/window/pallas_call | solution.py:517
  49.1 0.6 %copy.8 = f32[16,1024]{1,0:T(8,128)} copy(f32[16,1024]{1,0:T(8,128)S(1)} %window.1) | data formatting | bytes 131072

commit v5 on v4

--- a/solution.py
+++ b/solution.py
@@ -199,7 +199,7 @@
         drain(pbuf.at[1, g, 64:704], pr.at[g])
         for side in range(2):
             product = dot(pbuf[side, g, 64:704], ws[...])
-            qbuf[side, 0], qbuf[side, 1] = product[:, 0:128], product[:, 128:256]
+            qbuf[side, 0, 0:640], qbuf[side, 1, 0:640] = product[:, 0:128], product[:, 128:256]
         for side in range(2):
             even, odd = pl.ds(0, 320, stride=2), pl.ds(1, 320, stride=2)
             c = side * 256
@@ -530,7 +530,7 @@
             pltpu.VMEM((512, 512), BF16),
             pltpu.VMEM((256, 512), BF16),
             pltpu.VMEM((256, 512), BF16),
-            pltpu.VMEM((2, 2, 640, 128), F32),
+            pltpu.VMEM((2, 2, 656, 128), F32),
             pltpu.VMEM((320, 512), F32),
             pltpu.VMEM((288, 512), F32),
             pltpu.VMEM((272, 1024), F32),

time: 49.9 us -> 49.9 us (level)
  no operation moved by 1% of the time
where the time goes in v5:
time: 49.9 us; the launch traced here: 49.8 us
  Pallas kernels  49.1 us (98%)
  local copies, waits for them, and re-layouts  0.63 us (1%)
    pallas_call x1, Pallas kernels, body(): pl.pallas_call(kernel, out_shape=pltpu.VMEM((16, 1024), F32), in_specs=[p...  49.1 us

profile of v5, /device:TPU:1, one launch (start us, length us, event | category | flops | bytes accessed | tf_op | source)
XLA Modules:
  0.0 49.8 jit_solution(13526751606057237607)
XLA Ops:
  0.0 49.1 %window.1 = f32[16,1024]{1,0:T(8,128)S(1)} custom-call(bf16[8192,128]{1,0:T(8,128)(2,1)} %bitcast.2, bf16[2,128,128]{2,1,0:T(8,128)(2,1)} %steer_in.1, bf16[3,256,256]{2,1,0:T(8,128)(2,1)} %re_in.1, bf16[3,256,256]{2,1,0:T(8,128)(2,1)} %im_in.1, s32[3,2,128]{2,1,0:T(2,128)} %table_in.1, bf16[256,512]{1,0:T(8,128)(2,1)} %bitcast.3), custom_call_target="tpu_custom_call" | custom-call | flops 8000000000 | bytes 6000000 | tf_op jit(solution)/shard_map/window/pallas_call | solution.py:517
  49.1 0.6 %copy.8 = f32[16,1024]{1,0:T(8,128)} copy(f32[16,1024]{1,0:T(8,128)S(1)} %window.1) | data formatting | bytes 131072
